TPU v7x, 64 devices: a 2x2x8 block of a 4x4x8 slice. The times are simulated.
64 devices in a mesh: rep: 8 (over x, y, core), dp: 8 (over z).
Axes of the slice: x: 2, y: 2, z: 8, core: 2. Of those that a mesh axis runs over, the one named last changes fastest.
The devices are a block of a 4x4x8 slice.
Arguments:
- x: bfloat16 [64, 2048, 768], P(('rep', 'dp')), parts along dimension 0
- dy: bfloat16 [64, 2048, 768], P(('rep', 'dp')), parts along dimension 0
- w_gate: bfloat16 [2, 768, 1792], replicated
- w_up: bfloat16 [2, 768, 1792], replicated
- w_down: bfloat16 [2, 1792, 768], replicated
- m_w_gate: float32 [2, 768, 1792], P(None, 'dp')
- m_w_up: float32 [2, 768, 1792], P(None, 'dp')
- m_w_down: float32 [2, 1792, 768], P(None, 'dp')
- v_w_gate: float32 [2, 768, 1792], P(None, 'dp')
- v_w_up: float32 [2, 768, 1792], P(None, 'dp')
- v_w_down: float32 [2, 1792, 768], P(None, 'dp')
Outputs:
- output 1: bfloat16 [16, 768, 1792], P('rep'), parts along dimension 0
- output 2: bfloat16 [16, 768, 1792], P('rep'), parts along dimension 0
- output 3: bfloat16 [16, 1792, 768], P('rep'), parts along dimension 0
- output 4: float32 [16, 768, 1792], P('rep', 'dp'), parts along dimension 0
- output 5: float32 [16, 768, 1792], P('rep', 'dp'), parts along dimension 0
- output 6: float32 [16, 1792, 768], P('rep', 'dp'), parts along dimension 0
- output 7: float32 [16, 768, 1792], P('rep', 'dp'), parts along dimension 0
- output 8: float32 [16, 768, 1792], P('rep', 'dp'), parts along dimension 0
- output 9: float32 [16, 1792, 768], P('rep', 'dp'), parts along dimension 0
There are 8 independent parts. A program takes and returns all parts, laid end to end along the dimension named above; an argument that names none is the same for every part.
All inputs are finite; a program needn't handle non-finite values.
Results may differ from a plain program's by a relative error of at most 0.022.
Values are sent between devices in bfloat16 or wider.
A program may use at most 768 MiB of HBM per device.

v0:
```python
import jax
import jax.numpy as jnp
from jax import lax

NAMES = ("w_gate", "w_up", "w_down")


def matmul(a, w):
    return jnp.dot(a, w, preferred_element_type=jnp.float32).astype(jnp.bfloat16)


def normed(h):
    wide = h.astype(jnp.float32)
    scale = lax.rsqrt(jnp.mean(wide**2, -1, keepdims=True) + 1e-6)
    return (wide * scale).astype(jnp.bfloat16)


def layer(h, w):
    a = normed(h)
    gate = jnp.dot(a, w["w_gate"], preferred_element_type=jnp.float32)
    up = jnp.dot(a, w["w_up"], preferred_element_type=jnp.float32)
    return h + matmul((jax.nn.silu(gate) * up).astype(jnp.bfloat16), w["w_down"])


def adamw(w, m, v, g):
    m = 0.9 * m + 0.1 * g
    v = 0.95 * v + 0.05 * g * g
    step = m * lax.rsqrt(v + 1e-8) + 0.1 * w
    return (w - 0.02 * step).astype(jnp.bfloat16), m, v


def clipped(gradients, sum_of_squares, count):
    factor = jnp.minimum(1.0, 0.5 * lax.rsqrt(sum_of_squares / count + 1e-30))
    return [g * factor for g in gradients]


def stack(weights, h):
    for number in range(weights["w_gate"].shape[0]):
        h = layer(h, {name: w[number] for name, w in weights.items()})
    return h


def solution(mesh):
    groups = mesh.shape["rep"]

    def step(x, dy, *arrays):
        weights, m, v = (arrays[i : i + 3] for i in (0, 3, 6))
        x, dy = (t.reshape(groups, -1, *t.shape[1:]) for t in (x, dy))

        def of_a_group(x, dy):
            _, back = jax.vjp(lambda w: stack(w, x), dict(zip(NAMES, weights, strict=True)))
            by_weights = back(dy)[0]
            gradients = [by_weights[name].astype(jnp.float32) for name in NAMES]
            gradients = clipped(gradients, sum(jnp.sum(g * g) for g in gradients), sum(g.size for g in gradients))
            new = [adamw(w.astype(jnp.float32), m, v, g) for w, m, v, g in zip(weights, m, v, gradients, strict=True)]
            return tuple(one[which] for which in range(3) for one in new)

        return tuple(t.reshape(-1, *t.shape[2:]) for t in jax.vmap(of_a_group)(x, dy))

    return step
```

profile of v0, /device:TPU:28, one launch (start us, length us, event | category | flops | bytes accessed | tf_op | source)
XLA Modules:
  0.0 775.0 jit_solution(11979035069738786275)
XLA Ops:
  7.2 0.1 reduce-scatter.29.cloned.1.call-start
  7.3 2.7 fusion.35
  10.0 4.6 copy
  14.7 7.8 %fusion.77 = f32[2048,1792]{1,0:T(8,128)S(1)} fusion(bf16[2,768,1792]{2,1,0:T(8,128)(2,1)} %param, bf16[1,2048,768]{2,1,0:T(8,128)(2,1)S(1)} %copy-done.2, f32[2048]{0:T(1024)S(1)} %add_rsqrt_fusion), kind=kOutput, calls=%fused_computation.88 | convolution fusion | flops 5641863168 | bytes 20586496 | tf_op jit(solution)/vmap(jvp())/dot_general | solution.py:20
  22.5 13.2 %fusion.75 = f32[2048,1792]{1,0:T(8,128)S(1)} fusion(bf16[2,768,1792]{2,1,0:T(8,128)(2,1)} %param.3, bf16[1,2048,768]{2,1,0:T(8,128)(2,1)} %param.2, f32[2048]{0:T(1024)S(1)} %add_rsqrt_fusion), kind=kOutput, calls=%fused_computation.86 | convolution fusion | flops 5641863168 | bytes 20586496 | tf_op jit(solution)/vmap(jvp())/dot_general | solution.py:21
  35.7 7.4 fusion.26
  43.1 10.1 %fusion.39 = (f32[2048]{0:T(1024)S(1)}, bf16[1,1,2048,768]{2,3,1,0:T(8,128)(2,1)S(1)}) fusion(bf16[2048,1792]{1,0:T(8,128)(2,1)} %fusion.26, bf16[2,1792,768]{2,1,0:T(8,128)(2,1)} %param.4, bf16[1,2048,768]{1,2,0:T(8,128)(2,1)} %copy), kind=kOutput, calls=%fused_computation.56 | convolution fusion | flops 5645006848 | bytes 16392192 | tf_op jit(solution)/vmap(jvp())/dot_general | solution.py:9
  53.3 12.1 %fusion.67 = f32[2048,1792]{1,0:T(8,128)} fusion(bf16[2,768,1792]{2,1,0:T(8,128)(2,1)} %param, bf16[1,1,2048,768]{2,3,1,0:T(8,128)(2,1)S(1)} %get-tuple-element.10, f32[2048]{0:T(1024)S(1)} %bitcast.357), kind=kOutput, calls=%fused_computation.78 | convolution fusion | flops 5641863168 | bytes 20586496 | tf_op jit(solution)/vmap(jvp())/dot_general | solution.py:20
  65.4 11.0 %fusion.70 = f32[2048,1792]{1,0:T(8,128)} fusion(bf16[2,768,1792]{2,1,0:T(8,128)(2,1)} %param.3, bf16[1,1,2048,768]{2,3,1,0:T(8,128)(2,1)S(1)} %get-tuple-element.10, f32[2048]{0:T(1024)S(1)} %bitcast.358), kind=kOutput, calls=%fused_computation.81 | convolution fusion | flops 5641863168 | bytes 20586496 | tf_op jit(solution)/vmap(jvp())/dot_general | solution.py:21
  76.5 8.5 %convolution_convert_fusion.1 = bf16[2048,1792]{1,0:T(8,128)(2,1)} fusion(bf16[1,2048,768]{2,1,0:T(8,128)(2,1)S(1)} %copy-done.5, bf16[2,1792,768]{2,1,0:T(8,128)(2,1)S(1)} %bitcast.353), kind=kOutput, calls=%fused_computation.43 | convolution fusion | flops 5640814592 | bytes 13238272 | tf_op jit(solution)/vmap(transpose(jvp()))/dot_general | solution.py:9
  84.9 3.2 copy.1
  88.1 13.4 %fusion.6 = bf16[2048,1792]{1,0:T(8,128)(2,1)S(1)} fusion(f32[2048,1792]{1,0:T(8,128)} %fusion.67, f32[2048,1792]{1,0:T(8,128)} %fusion.70, bf16[2048,1792]{1,0:T(8,128)(2,1)} %convolution_convert_fusion.1), kind=kLoop, calls=%fused_computation.11 | loop fusion | flops 44040192 | bytes 44040192
  101.6 2.9 copy-done.3
  104.5 7.6 convolution_convert_fusion.2
  112.2 13.1 %fusion.41 = (f32[2048]{0:T(1024)S(1)}, bf16[2048,768]{0,1:T(8,128)(2,1)}) fusion(bf16[1,1,2048,768]{2,3,1,0:T(8,128)(2,1)S(1)} %copy-done.9, bf16[2048,768]{0,1:T(8,128)(2,1)S(1)} %convolution_convert_fusion.2, bf16[2,768,1792]{2,1,0:T(8,128)(2,1)} %param.3, bf16[2048,1792]{1,0:T(8,128)(2,1)} %convolution_convert_fusion.1, f32[2048,1792]{1,0:T(8,128)} %fusion.67), kind=kOutput, calls=%fused_computation.58 | convolution fusion | flops 5668599808 | bytes 34217984 | tf_op jit(solution)/vmap(transpose(jvp()))/dot_general | solution.py:21
  125.2 4.1 fusion.60
  129.4 1.7 copy-done.11
  131.0 10.0 %convolution_bitcast_fusion = f32[1,1792,768]{2,1,0:T(8,128)} fusion(bf16[2048,1792]{1,0:T(8,128)(2,1)} %fusion.26, bf16[2048,768]{0,1:T(8,128)(2,1)S(1)} %fusion.60), kind=kOutput, calls=%fused_computation.63 | convolution fusion | flops 5637144576 | bytes 15990784 | tf_op jit(solution)/vmap(transpose(jvp()))/dot_general | solution.py:9
  141.0 0.1 reduce-scatter.27.cloned.1.call-start
  141.1 1.8 copy-done.6
  142.9 14.4 %fusion.42 = f32[1,1792,768]{2,1,0:T(8,128)} fusion(f32[2048,1792]{1,0:T(8,128)} %fusion.70, f32[2048,1792]{1,0:T(8,128)} %fusion.67, bf16[1,2048,768]{2,1,0:T(8,128)(2,1)S(1)} %copy-done.6), kind=kOutput, calls=%fused_computation.60 | convolution fusion | flops 5659164672 | bytes 38010880 | tf_op jit(solution)/vmap(transpose(jvp()))/dot_general | solution.py:9
  157.2 0.1 reduce-scatter.27.cloned.1.call-update
  157.3 0.1 reduce-scatter.25.cloned.1.call-start
  157.4 8.8 %convolution_convert_fusion = bf16[2048,1792]{1,0:T(8,128)(2,1)S(1)} fusion(bf16[2048,768]{0,1:T(8,128)(2,1)} %copy-done.11, bf16[2,1792,768]{2,1,0:T(8,128)(2,1)} %param.4), kind=kOutput, calls=%fused_computation.42 | convolution fusion | flops 5640814592 | bytes 13238272 | tf_op jit(solution)/vmap(transpose(jvp()))/dot_general | solution.py:9
  166.2 3.0 copy-done.17
  169.2 11.9 %fusion.48 = f32[1,768,1792]{2,1,0:T(8,128)} fusion(bf16[2048,1792]{1,0:T(8,128)(2,1)S(1)} %convolution_convert_fusion, f32[2048,1792]{1,0:T(8,128)} %copy-done, bf16[1,2048,768]{1,2,0:T(8,128)(2,1)S(1)} %copy-done.7, f32[2048]{0:T(1024)S(1)} %copy-done.15), kind=kOutput, calls=%fused_computation.62 | convolution fusion | flops 5663883264 | bytes 30679040 | tf_op jit(solution)/vmap(transpose(jvp()))/dot_general | solution.py:21
  181.2 0.1 reduce-scatter.23.cloned.1.call-start
  181.3 13.9 %fusion.45 = f32[1,768,1792]{2,1,0:T(8,128)} fusion(bf16[2048,1792]{1,0:T(8,128)(2,1)} %convolution_convert_fusion.1, f32[2048,1792]{1,0:T(8,128)} %fusion.67, bf16[1,1,2048,768]{2,3,1,0:T(8,128)(2,1)} %copy-done.8, f32[2048]{0:T(1024)S(1)} %bitcast.360), kind=kOutput, calls=%fused_computation.61 | convolution fusion | flops 5663883264 | bytes 30679040 | tf_op jit(solution)/vmap(transpose(jvp()))/dot_general | solution.py:21
  195.3 0.1 reduce-scatter.21.cloned.1.call-start
  195.4 17.5 %fusion.51 = f32[1,768,1792]{2,1,0:T(8,128)} fusion(f32[2048,1792]{1,0:T(8,128)} %copy-done, f32[2048,1792]{1,0:T(8,128)} %copy-done.1, bf16[2048,1792]{1,0:T(8,128)(2,1)} %copy-done.17, bf16[1,2048,768]{1,2,0:T(8,128)(2,1)S(1)} %copy-done.7, f32[2048]{0:T(1024)S(1)} %copy-done.15), kind=kOutput, calls=%fused_computation.65 | convolution fusion | flops 5682233344 | bytes 45359104 | tf_op jit(solution)/vmap(transpose(jvp()))/dot_general | solution.py:20
  212.9 0.1 reduce-scatter.19.cloned.1.call-start
  213.0 1.8 copy-done.10
  214.8 10.6 %convolution_bitcast_fusion.1 = f32[1,768,1792]{2,1,0:T(8,128)} fusion(bf16[2048,1792]{1,0:T(8,128)(2,1)} %copy-done.3, bf16[1,1,2048,768]{2,3,1,0:T(8,128)(2,1)S(1)} %copy-done.10, f32[2048]{0:T(1024)S(1)} %bitcast.361), kind=kOutput, calls=%fused_computation.64 | convolution fusion | flops 5641863168 | bytes 15998976 | tf_op jit(solution)/vmap(transpose(jvp()))/dot_general | solution.py:20
  225.5 0.1 all-gather.14.cloned.1.call-start
  225.6 0.5 copy-done.16
  226.1 0.6 dynamic-slice
  227.3 1.1 convert_bitcast_fusion.3
  228.5 46.1 %reduce-scatter.27.cloned.1.call-done = f32[1,224,768]{2,1,0:T(8,128)} async-done(((f32[1,1792,768]{2,1,0:T(8,128)}), f32[1,224,768]{2,1,0:T(8,128)}) %reduce-scatter.27.cloned.1.call-update) | async-done | bytes 688144
  274.6 1.1 convert_bitcast_fusion.4
  275.8 1.0 fusion.110
  276.7 63.9 %reduce-scatter.25.cloned.1.call-done = f32[1,96,1792]{2,1,0:T(8,128)} async-done(((f32[1,768,1792]{2,1,0:T(8,128)}), f32[1,96,1792]{2,1,0:T(8,128)}) %reduce-scatter.25.cloned.1.call-update) | async-done | bytes 688144
  340.6 1.1 convert_bitcast_fusion.5
  341.8 64.1 %reduce-scatter.23.cloned.1.call-done = f32[1,96,1792]{2,1,0:T(8,128)} async-done(((f32[1,768,1792]{2,1,0:T(8,128)}), f32[1,96,1792]{2,1,0:T(8,128)}) %reduce-scatter.23.cloned.1.call-update) | async-done | bytes 688144
  405.9 1.1 convert_bitcast_fusion.6
  407.1 1.0 fusion.109
  408.0 63.8 %reduce-scatter.21.cloned.1.call-done = f32[1,96,1792]{2,1,0:T(8,128)} async-done(((f32[1,768,1792]{2,1,0:T(8,128)}), f32[1,96,1792]{2,1,0:T(8,128)}) %reduce-scatter.21.cloned.1.call-update) | async-done | bytes 688144
  471.8 1.1 convert_bitcast_fusion.7
  472.9 64.7 %reduce-scatter.19.cloned.1.call-done = f32[1,96,1792]{2,1,0:T(8,128)} async-done(((f32[1,768,1792]{2,1,0:T(8,128)}), f32[1,96,1792]{2,1,0:T(8,128)}) %reduce-scatter.19.cloned.1.call-update) | async-done | bytes 688144
  537.6 1.1 convert_bitcast_fusion.8
  538.8 1.0 fusion.108
  541.7 16.7 %all-reduce.16 = f32[1]{0:T(128)} all-reduce(f32[1]{0:T(128)} %bitcast.50), channel_id=5, replica_groups=mesh['rep'=8,'dp'=8] {'dp'}, use_global_device_ids=true, to_apply=%region_3.4.clone | all-reduce | flops 1 | bytes 8 | tf_op jit(solution)/vmap()/reduce_sum | solution.py:54
  559.1 4.1 fusion.129
  563.2 0.1 all-gather.12.cloned.1.call-start
  563.3 4.5 fusion.130
  567.9 0.1 all-gather.10.cloned.1.call-start
  568.0 4.0 fusion.131
  572.1 54.8 %all-gather.14.cloned.1.call-done = bf16[1,2,1792,768]{3,2,1,0:T(8,128)(2,1)} async-done(((bf16[1,2,224,768]{3,2,1,0:T(8,128)(2,1)}), bf16[1,2,1792,768]{3,2,1,0:T(8,128)(2,1)}) %all-gather.14.cloned.1.call-update) | async-done | bytes 5505040 | tf_op jit(solution)/reshape | solution.py:58
  626.8 64.4 %all-gather.12.cloned.1.call-done = bf16[1,2,768,1792]{3,2,1,0:T(8,128)(2,1)} async-done(((bf16[1,2,96,1792]{3,2,1,0:T(8,128)(2,1)}), bf16[1,2,768,1792]{3,2,1,0:T(8,128)(2,1)}) %all-gather.12.cloned.1.call-update) | async-done | bytes 5505040 | tf_op jit(solution)/reshape | solution.py:58
  691.3 64.4 %all-gather.10.cloned.1.call-done = bf16[1,2,768,1792]{3,2,1,0:T(8,128)(2,1)} async-done(((bf16[1,2,96,1792]{3,2,1,0:T(8,128)(2,1)}), bf16[1,2,768,1792]{3,2,1,0:T(8,128)(2,1)}) %all-gather.10.cloned.1.call-update) | async-done | bytes 5505040 | tf_op jit(solution)/reshape | solution.py:58
  755.7 5.9 copy.5
  761.6 2.8 copy.6
  764.4 0.1 slice-done
  764.5 1.1 slice-done.1
  765.6 2.4 copy.7
  (51 shorter events, 0.6 us)
Async XLA Ops:
  7.2 7.5 copy-start.2
  7.2 220.1 %reduce-scatter.29.cloned.1.call-start = ((), (), s32[]{:S(2)}) async-start(), calls=%async_computation.14 | async-start | bytes 6193152
  14.6 7.9 %copy-start.14 = (f32[2048]{0:T(1024)}, f32[2048]{0:T(1024)S(1)}, u32[]{:S(2)}) copy-start(f32[2048]{0:T(1024)S(1)} %add_rsqrt_fusion) | copy-start | bytes 24580
  22.5 13.2 %copy-start = (f32[2048,1792]{1,0:T(8,128)}, f32[2048,1792]{1,0:T(8,128)S(1)}, u32[]{:S(2)}) copy-start(f32[2048,1792]{1,0:T(8,128)S(1)} %fusion.77) | copy-start | bytes 44040196
  35.7 7.4 copy-start.1
  43.1 33.3 %slice-start.2 = ((s8[5505024]{0:T(1024)(128)(4,1)}), s8[4194304]{0:T(1024)(128)(4,1)S(1)}, s32[]{:S(2)}) async-start(s8[5505024]{0:T(1024)(128)(4,1)} %bitcast.352), calls=%async_computation.17 | async-start | bytes 8388608
  53.2 12.2 %copy-start.8 = (bf16[1,1,2048,768]{2,3,1,0:T(8,128)(2,1)}, bf16[1,1,2048,768]{2,3,1,0:T(8,128)(2,1)S(1)}, u32[]{:S(2)}) copy-start(bf16[1,1,2048,768]{2,3,1,0:T(8,128)(2,1)S(1)} %get-tuple-element.10) | copy-start | bytes 9437188
  53.3 23.2 %slice-start.3 = ((s8[5505024]{0:T(1024)(128)(4,1)}), s8[1310720]{0:T(1024)(128)(4,1)S(1)}, s32[]{:S(2)}) async-start(s8[5505024]{0:T(1024)(128)(4,1)} %bitcast.352), calls=%async_computation.18 | async-start | bytes 2621440
  65.4 11.0 %copy-start.5 = (bf16[1,2048,768]{2,1,0:T(8,128)(2,1)S(1)}, bf16[1,2048,768]{2,1,0:T(8,128)(2,1)}, u32[]{:S(2)}) copy-start(bf16[1,2048,768]{2,1,0:T(8,128)(2,1)} %param.5) | copy-start | bytes 9437188
  101.6 3.0 copy-start.3
  104.5 7.6 copy-start.9
  129.3 1.7 copy-start.11
  141.0 1.9 copy-start.6
  141.0 133.6 %reduce-scatter.27.cloned.1.call-start = ((), (), s32[]{:S(2)}) async-start(), calls=%async_computation.13 | async-start | bytes 6193152
  157.3 11.9 %copy-start.7 = (bf16[1,2048,768]{1,2,0:T(8,128)(2,1)S(1)}, bf16[1,2048,768]{1,2,0:T(8,128)(2,1)}, u32[]{:S(2)}) copy-start(bf16[1,2048,768]{1,2,0:T(8,128)(2,1)} %copy) | copy-start | bytes 9437188
  157.3 11.9 %copy-start.15 = (f32[2048]{0:T(1024)S(1)}, f32[2048]{0:T(1024)}, u32[]{:S(2)}) copy-start(f32[2048]{0:T(1024)} %copy-done.14) | copy-start | bytes 24580
  157.3 183.3 %reduce-scatter.25.cloned.1.call-start = ((), (), s32[]{:S(2)}) async-start(), calls=%async_computation.12 | async-start | bytes 6193152
  166.2 3.0 copy-start.17
  181.2 224.7 %reduce-scatter.23.cloned.1.call-start = ((), (), s32[]{:S(2)}) async-start(), calls=%async_computation.11 | async-start | bytes 6193152
  195.3 276.5 %reduce-scatter.21.cloned.1.call-start = ((), (), s32[]{:S(2)}) async-start(), calls=%async_computation.10 | async-start | bytes 6193152
  212.9 1.9 copy-start.10
  212.9 324.7 %reduce-scatter.19.cloned.1.call-start = ((), (), s32[]{:S(2)}) async-start(), calls=%async_computation.9 | async-start | bytes 6193152
  225.4 0.7 copy-start.16
  225.5 333.6 %copy-start.12 = (f32[2,224,768]{2,1,0:T(8,128)S(1)}, f32[2,224,768]{2,1,0:T(8,128)}, u32[]{:S(2)}) copy-start(f32[2,224,768]{2,1,0:T(8,128)} %param.10) | copy-start | bytes 4128772
  225.5 401.3 %all-gather.14.cloned.1.call-start = ((), (), s32[]{:S(2)}) async-start(), calls=%async_computation.8 | async-start | bytes 6193152 | tf_op jit(solution)/reshape | solution.py:58
  563.1 4.8 copy-start.13
  563.2 128.1 %all-gather.12.cloned.1.call-start = ((), (), s32[]{:S(2)}) async-start(), calls=%async_computation.7 | async-start | bytes 6193152 | tf_op jit(solution)/reshape | solution.py:58
  567.9 187.8 %all-gather.10.cloned.1.call-start = ((), (), s32[]{:S(2)}) async-start(), calls=%async_computation.6 | async-start | bytes 6193152 | tf_op jit(solution)/reshape | solution.py:58
  755.7 5.9 copy-start.4
  755.7 8.8 %slice-start = ((s8[5505024]{0:T(1024)(128)(4,1)}), s8[4194304]{0:T(1024)(128)(4,1)S(1)}, s32[]{:S(2)}) async-start(s8[5505024]{0:T(1024)(128)(4,1)} %bitcast.347), calls=%async_computation.15 | async-start | bytes 8388608
  761.6 4.0 slice-start.1
Sparse Core Ops, SparseCore 0:
  141.2 67.9 reduce-scatter.28
  211.6 63.0 reduce-scatter.26
  277.6 63.0 reduce-scatter.24
  342.9 63.0 reduce-scatter.22
  408.7 63.0 reduce-scatter.20
  474.6 63.0 reduce-scatter.18
  563.3 63.4 all-gather.13
  629.0 62.2 all-gather.11
  693.4 62.2 all-gather.9
where the time goes:
time: 785 us; the launch traced here: 775 us
  waiting for transfers between devices  487 us (62%)
  matrix products  171 us (22%)
  other arithmetic  50.1 us (6%)
  local copies, waits for them, and re-layouts  32.4 us (4%)
  between operations  17.9 us (2%)
  blocking collectives  16.7 us (2%)
    unnamed x15, waiting for transfers between devices  303 us
    reshape x3, waiting for transfers between devices, step(): t.reshape(-1, *t.shape[2:])  184 us
    dot_general x5, matrix products, layer(): up = jnp.dot(a, w['w_up'], preferred_element_type=jnp.float32)  63.1 us
    dot_general x5, matrix products, layer(): gate = jnp.dot(a, w['w_gate'], preferred_element_type=jnp.float32)  55.7 us
    dot_general x5, matrix products, matmul(): jnp.dot(a, w, preferred_element_type=jnp.float32).astype(jnp.bfloat16)  51.7 us
    unnamed x49, local copies, waits for them, and re-layouts  31.8 us
    unnamed x5, other arithmetic  25 us
    reduce_sum x1, blocking collectives, of_a_group(): jnp.sum(g * g)  16.7 us
  transfers between devices with their start and end apart: 9, of which 8 were waited for; matrix products, arithmetic and copies ran while one was open for 12% of the time, Pallas kernels for 0%

commit v1 on v0

v1 whole, which is shorter than its diff:
```python
import functools

import jax
import jax.numpy as jnp
from jax import lax
from jax.experimental import pallas as pl
from jax.experimental.pallas import tpu as pltpu
from jax.sharding import PartitionSpec as P

NAMES = ("w_gate", "w_up", "w_down")
MESH = pl.DeviceIdType.MESH
F32, BF16 = jnp.float32, jnp.bfloat16
COLS = 256
VMEM_MAX = 67_043_328


def matmul(a, w):
    return jnp.dot(a, w, preferred_element_type=jnp.float32).astype(jnp.bfloat16)


def normed(h):
    wide = h.astype(jnp.float32)
    scale = lax.rsqrt(jnp.mean(wide**2, -1, keepdims=True) + 1e-6)
    return (wide * scale).astype(jnp.bfloat16)


def layer(h, w):
    a = normed(h)
    gate = jnp.dot(a, w["w_gate"], preferred_element_type=jnp.float32)
    up = jnp.dot(a, w["w_up"], preferred_element_type=jnp.float32)
    return h + matmul((jax.nn.silu(gate) * up).astype(jnp.bfloat16), w["w_down"])


def stack(weights, h):
    for number in range(weights["w_gate"].shape[0]):
        h = layer(h, {name: w[number] for name, w in weights.items()})
    return h


class Plan:
    def __init__(self, n, layers, d, ff):
        self.n, self.layers, self.d, self.ff = n, layers, d, ff
        self.rows = d // n
        self.block = ff // n
        self.wide = d // COLS
        self.strip = self.rows // self.wide
        self.chunks = ff // COLS
        self.strips = self.block // self.strip
        self.hops = n // 2
        assert n % 2 == 0 and d % COLS == 0 and ff % COLS == 0 and self.rows % (16 * self.wide) == 0
        assert self.block % self.strip == 0
        subs = []
        late = []
        for l in reversed(range(layers)):
            for c in range(self.chunks):
                subs += [("gate", l, c), ("up", l, c)]
            downs = late + [("down", l, s) for s in range(self.strips)]
            late = downs[len(downs) // 2 * 2 :]
            subs += downs[: len(downs) // 2 * 2]
        assert not late
        self.subs = subs
        self.units = len(subs) // 2

    def each(self):
        for i, (kind, l, k) in enumerate(self.subs):
            yield i // 2, i % 2, kind, l, k

    def views(self, p, half, kind, l, k, own, arrays, lead=()):
        gate, up, down = arrays
        if kind != "down":
            array = gate if kind == "gate" else up
            yield own.at[(p, *lead, half)], array.at[(l, *lead, slice(None), pl.ds(k * COLS, COLS))]
        else:
            for c in range(self.wide):
                yield (
                    own.at[(p, *lead, half, pl.ds(c * self.strip, self.strip))],
                    down.at[(l, *lead, pl.ds(k * self.strip, self.strip), pl.ds(c * COLS, COLS))],
                )


def comm_kernel(plan, count, grads, weights, moments_m, moments_v, own, m, v, landing, w, squares, sums, local_sems, send, recv, send_s, recv_s):
    n, hops, units = plan.n, plan.hops, plan.units
    me = lax.axis_index("dp")
    right, left = lax.rem(me + 1, n), lax.rem(me + n - 1, n)

    def at(k):
        return lax.rem(me + k + n, n)

    barrier = pltpu.get_barrier_semaphore()
    for k in range(1, n):
        pl.semaphore_signal(barrier, inc=1, device_id={"dp": at(k)}, device_id_type=MESH)

    every = slice(None)
    for p, half, kind, l, k in plan.each():
        for inside, outside in plan.views(p, half, kind, l, k, own, grads, (every,)):
            pltpu.make_async_copy(outside, inside, local_sems.at[0]).start()
    for p, half, kind, l, k in plan.each():
        for inside, outside in plan.views(p, half, kind, l, k, w, [a.at[:, me] for a in weights]):
            pltpu.make_async_copy(outside, inside, local_sems.at[1]).start()
        for inside, outside in plan.views(p, half, kind, l, k, m, moments_m):
            pltpu.make_async_copy(outside, inside, local_sems.at[2]).start()
        for inside, outside in plan.views(p, half, kind, l, k, v, moments_v):
            pltpu.make_async_copy(outside, inside, local_sems.at[3]).start()
    pl.semaphore_wait(barrier, n - 1)
    pltpu.make_async_copy(own, own, local_sems.at[0]).wait()

    def hop(p, h, d):
        b = at(hops - h) if d == 0 else at(h - hops)
        if h == 0:
            source, target = own.at[p, b, d], landing.at[p, d, 0, d]
        else:
            source, target = own.at[p, b], landing.at[p, d, h]
        return pltpu.make_async_remote_copy(
            source, target, send.at[p, h, d], recv.at[p, h, d], device_id={"dp": right if d == 0 else left}, device_id_type=MESH
        )

    for h in range(hops):

        @pl.loop(0, units)
        def _(p, h=h):
            for d in (0, 1):
                if h > 0:
                    hop(p, h - 1, d).wait_recv()
                    b = at(hops - h) if d == 0 else at(h - hops)
                    if h == 1:
                        own[p, b, d] = (own[p, b, d].astype(F32) + landing[p, d, 0, d].astype(F32)).astype(BF16)
                    else:
                        own[p, b] = (own[p, b].astype(F32) + landing[p, d, h - 1].astype(F32)).astype(BF16)
                hop(p, h, d).start()

    squares[...] = jnp.zeros_like(squares)

    @pl.loop(0, units)
    def _(p):
        for d in (0, 1):
            hop(p, hops - 1, d).wait_recv()
        for half in (0, 1):
            g = own[p, me, half].astype(F32) + landing[p, 0, hops - 1, half].astype(F32) + landing[p, 1, hops - 1, half].astype(F32)
            g = g.astype(BF16)
            own[p, me, half] = g
            g = g.astype(F32)
            squares[...] += g * g
        for h in range(hops):
            for d in (0, 1):
                hop(p, h, d).wait_send()

    part = jnp.sum(squares[...].reshape(-1, 8, COLS), axis=0)
    part = sum(part[:, i * 128 : (i + 1) * 128] for i in range(COLS // 128))
    sums[0] = part

    def tell(k):
        return pltpu.make_async_remote_copy(
            sums.at[0], sums.at[k], send_s.at[k], recv_s.at[k], device_id={"dp": at(k)}, device_id_type=MESH
        )

    for k in range(1, n):
        tell(k).start()
    pltpu.make_async_copy(w, w, local_sems.at[1]).wait()
    pltpu.make_async_copy(m, m, local_sems.at[2]).wait()
    pltpu.make_async_copy(v, v, local_sems.at[3]).wait()
    for k in range(1, n):
        tell(k).wait_recv()
    total = jnp.sum(jnp.sum(sums[...], axis=0), axis=(0, 1), keepdims=True)
    factor = jnp.minimum(1.0, 0.5 * lax.rsqrt(total / count + 1e-30))
    for k in range(1, n):
        tell(k).wait_send()

    def pass_on(p, h, d):
        b = at(-h) if d == 0 else at(h)
        ref = own.at[p, b] if h < hops - 1 else own.at[p, b, d]
        return pltpu.make_async_remote_copy(
            ref, ref, send.at[p, h, d], recv.at[p, h, d], device_id={"dp": right if d == 0 else left}, device_id_type=MESH
        )

    @pl.loop(0, units)
    def _(p):
        for half in (0, 1):
            g = own[p, me, half].astype(F32) * factor
            new_m = 0.9 * m[p, half] + 0.1 * g
            new_v = 0.95 * v[p, half] + 0.05 * g * g
            old = w[p, half].astype(F32)
            step = new_m * lax.rsqrt(new_v + 1e-8) + 0.1 * old
            own[p, me, half] = (old - 0.02 * step).astype(BF16)
            m[p, half] = new_m
            v[p, half] = new_v
        for d in (0, 1):
            pass_on(p, 0, d).start()

    for h in range(1, hops):

        @pl.loop(0, units)
        def _(p, h=h):
            for d in (0, 1):
                pass_on(p, h - 1, d).wait_recv()
                pass_on(p, h, d).start()

    @pl.loop(0, units)
    def _(p):
        for d in (0, 1):
            pass_on(p, hops - 1, d).wait_recv()
            for h in range(hops):
                pass_on(p, h, d).wait_send()


def place_kernel(plan, own, m, v, weights, new_m, new_v, sems):
    every = slice(None)
    copies = []
    for p, half, kind, l, k in plan.each():
        for inside, outside in plan.views(p, half, kind, l, k, own, weights, (every,)):
            copies.append((inside, outside, 0))
        for inside, outside in plan.views(p, half, kind, l, k, m, new_m):
            copies.append((inside, outside, 1))
        for inside, outside in plan.views(p, half, kind, l, k, v, new_v):
            copies.append((inside, outside, 2))
    for inside, outside, s in copies:
        pltpu.make_async_copy(inside, outside, sems.at[s]).start()
    for inside, outside, s in copies:
        pltpu.make_async_copy(inside, outside, sems.at[s]).wait()


def solution(mesh):
    n = mesh.shape["dp"]

    def step(x, dy, *arrays):
        weights, m, v = (arrays[i : i + 3] for i in (0, 3, 6))
        layers, d, ff = weights[0].shape
        plan = Plan(n, layers, d, ff)
        _, back = jax.vjp(lambda w: stack(w, x[0]), dict(zip(NAMES, weights, strict=True)))
        by_weights = back(dy[0])[0]
        grads = [by_weights[name].reshape(layers, n, -1, by_weights[name].shape[-1]) for name in NAMES]
        blocks = [w.reshape(layers, n, -1, w.shape[-1]) for w in weights]
        count = float(sum(w.size for w in weights))
        units, rows = plan.units, plan.rows
        anywhere = pl.BlockSpec(memory_space=pl.ANY)

        def body(*refs):
            grads, weights, m, v = (refs[i : i + 3] for i in (0, 3, 6, 9))
            comm_kernel(plan, count, grads, weights, m, v, *refs[12:])

        out_shape = [
            pltpu.VMEM((units, n, 2, rows, COLS), BF16),
            pltpu.VMEM((units, 2, rows, COLS), F32),
            pltpu.VMEM((units, 2, rows, COLS), F32),
        ]
        own, new_m, new_v = pl.pallas_call(
            body,
            out_shape=out_shape,
            in_specs=[anywhere] * 12,
            out_specs=[pl.BlockSpec(memory_space=pltpu.VMEM)] * 3,
            scratch_shapes=[
                pltpu.VMEM((units, 2, plan.hops, 2, rows, COLS), BF16),
                pltpu.VMEM((units, 2, rows, COLS), BF16),
                pltpu.VMEM((rows, COLS), F32),
                pltpu.VMEM((n, 8, 128), F32),
                pltpu.SemaphoreType.DMA((4,)),
                pltpu.SemaphoreType.DMA((units, plan.hops, 2)),
                pltpu.SemaphoreType.DMA((units, plan.hops, 2)),
                pltpu.SemaphoreType.DMA((n,)),
                pltpu.SemaphoreType.DMA((n,)),
            ],
            compiler_params=pltpu.CompilerParams(collective_id=0, has_side_effects=True, vmem_limit_bytes=24 * 2**20),
            name="exchange",
        )(*grads, *blocks, *m, *v)

        def place(*refs):
            place_kernel(plan, *refs[:3], refs[3:6], refs[6:9], refs[9:12], refs[12])

        shapes = [jax.ShapeDtypeStruct(b.shape, b.dtype) for b in blocks]
        shapes += [jax.ShapeDtypeStruct(t.shape, t.dtype) for t in (*m, *v)]
        out = pl.pallas_call(
            place,
            out_shape=shapes,
            in_specs=[pl.BlockSpec(memory_space=pltpu.VMEM)] * 3,
            out_specs=[anywhere] * 9,
            scratch_shapes=[pltpu.SemaphoreType.DMA((3,))],
            compiler_params=pltpu.CompilerParams(vmem_limit_bytes=2**20),
            name="place",
        )(own, new_m, new_v)
        return tuple(o.reshape(w.shape) for o, w in zip(out[:3], weights)) + tuple(out[3:])

    rows = P(None, "dp", None)
    seq = P(("rep", "dp"), None, None)
    return jax.shard_map(
        step,
        mesh=mesh,
        in_specs=(seq, seq, P(), P(), P()) + (rows,) * 6,
        out_specs=(P("rep"),) * 3 + (P("rep", "dp", None),) * 6,
        check_vma=False,
    )
```

time: 785 us -> 558 us (0.71)
  waiting for transfers between devices: 487 us -> 0 us
  Pallas kernels: 0 us -> 341 us
  other arithmetic: 50.1 us -> 17.2 us
  local copies, waits for them, and re-layouts: 32.4 us -> 6.58 us
  between operations: 17.9 us -> 1.14 us
  blocking collectives: 16.7 us -> 0 us
  matrix products: 171 us -> 185 us
    pallas_call x0 -> x2, Pallas kernels: none -> 341 us  [the longest x1 332 us: step(): pl.pallas_call(body, out_shape=out_shape, in_specs=[anywhere] * 12, out_s...]
    unnamed x15 -> x0, waiting for transfers between devices: 303 us -> none
    reshape x3 -> x0, waiting for transfers between devices: 184 us -> none  [step(): t.reshape(-1, *t.shape[2:])]
    unnamed x49 -> x46, local copies, waits for them, and re-layouts: 31.8 us -> 6.58 us
    unnamed x5 -> x3, other arithmetic: 25 us -> 0.01 us
    reduce_sum x1 -> x0, blocking collectives: 16.7 us -> none  [of_a_group(): jnp.sum(g * g)]
    add_any x0 -> x4, other arithmetic: none -> 16.5 us  [the longest x3 11.5 us: stack(): h = layer(h, {name: w[number] for name, w in weights.items()})]
    dot_general x5, matrix products: 55.7 us -> 72.2 us  [layer(): gate = jnp.dot(a, w['w_gate'], preferred_element_type=jnp.float32)]
  transfers between devices with their start and end apart: 9 -> 0, of which waited for: 8 -> 0; matrix products, arithmetic and copies ran while one was open for 12% -> 0% of each run, Pallas kernels for 0% -> 0%
where the time goes in v1:
time: 558 us; the launch traced here: 550 us
  Pallas kernels  341 us (61%)
  matrix products  185 us (33%)
  other arithmetic  17.2 us (3%)
  local copies, waits for them, and re-layouts  6.58 us (1%)
    pallas_call x1, Pallas kernels, step(): pl.pallas_call(body, out_shape=out_shape, in_specs=[anywhere] * 12, out_s...  332 us
    dot_general x5, matrix products, layer(): gate = jnp.dot(a, w['w_gate'], preferred_element_type=jnp.float32)  72.2 us
    dot_general x5, matrix products, layer(): up = jnp.dot(a, w['w_up'], preferred_element_type=jnp.float32)  63.8 us
    dot_general x5, matrix products, matmul(): jnp.dot(a, w, preferred_element_type=jnp.float32).astype(jnp.bfloat16)  48.8 us
    add_any x3, other arithmetic, stack(): h = layer(h, {name: w[number] for name, w in weights.items()})  11.5 us

profile of v1, /device:TPU:28, one launch (start us, length us, event | category | flops | bytes accessed | tf_op | source)
XLA Modules:
  0.0 550.3 jit_solution(10229544550105459595)
XLA Ops:
  0.6 3.2 copy.20
  3.8 0.0 copy-start.4
  3.8 0.0 slice-start
  3.9 0.7 fusion.15
  4.5 0.0 copy-start.14
  4.5 0.0 slice-start.1
  4.6 12.9 %fusion.56 = f32[2048,1792]{1,0:T(8,128)} fusion(bf16[2,768,1792]{2,1,0:T(8,128)(2,1)} %param.13, bf16[1,2048,768]{2,1,0:T(8,128)(2,1)} %param.11, f32[2048]{0:T(1024)S(1)} %add_rsqrt_fusion), kind=kOutput, calls=%fused_computation.75 | convolution fusion | flops 5641863168 | bytes 20586496 | tf_op jit(solution)/shard_map/jvp()/dot_general | solution.py:29
  17.4 0.0 copy-done.14
  17.4 0.0 slice-done
  17.4 0.0 slice-done.1
  17.5 16.3 %multiply_convert_fusion.1 = (bf16[2048,1792]{1,0:T(8,128)(2,1)}, f32[2048,1792]{1,0:T(8,128)}) fusion(f32[2048,1792]{1,0:T(8,128)} %fusion.56, bf16[2,768,1792]{2,1,0:T(8,128)(2,1)S(1)} %bitcast.91, bf16[1,2048,768]{2,1,0:T(8,128)(2,1)} %param.11, f32[2048]{0:T(1024)S(1)} %add_rsqrt_fusion), kind=kOutput, calls=%fused_computation.17 | convolution fusion | flops 5663883264 | bytes 42606592 | tf_op jit(solution)/shard_map/jvp()/dot_general | solution.py:30
  33.7 0.0 copy-done.4
  33.8 0.0 slice-start.2
  33.8 9.5 %fusion.19 = (f32[2048]{0:T(1024)S(1)}, bf16[2048,768]{0,1:T(8,128)(2,1)S(1)}) fusion(bf16[2048,1792]{1,0:T(8,128)(2,1)} %get-tuple-element.33, bf16[2,1792,768]{2,1,0:T(8,128)(2,1)} %param.15, bf16[1,2048,768]{1,2,0:T(8,128)(2,1)S(1)} %copy.20), kind=kOutput, calls=%fused_computation.37 | convolution fusion | flops 5645006848 | bytes 16392192 | tf_op jit(solution)/shard_map/jvp()/dot_general | solution.py:18
  43.3 0.0 copy-start.7
  43.3 0.0 copy-start.12
  43.3 0.0 slice-start.3
  43.3 0.0 copy-start.6
  43.4 9.4 %fusion.49 = f32[2048,1792]{1,0:T(8,128)} fusion(bf16[2,768,1792]{2,1,0:T(8,128)(2,1)S(1)} %bitcast.91, bf16[2048,768]{0,1:T(8,128)(2,1)S(1)} %get-tuple-element.36, f32[2048]{0:T(1024)S(1)} %fusion.79), kind=kOutput, calls=%fused_computation.68 | convolution fusion | flops 5641863168 | bytes 20586496 | tf_op jit(solution)/shard_map/jvp()/dot_general | solution.py:30
  52.7 0.0 copy-done.7
  52.7 0.0 copy-done.12
  52.7 0.0 slice-done.2
  52.7 0.0 slice-done.3
  52.8 0.0 copy-done.6
  52.8 8.1 %convolution_convert_fusion.1 = bf16[2048,1792]{1,0:T(8,128)(2,1)} fusion(bf16[1,2048,768]{2,1,0:T(8,128)(2,1)S(1)} %copy-done.6, bf16[2,1792,768]{2,1,0:T(8,128)(2,1)S(1)} %bitcast.94), kind=kOutput, calls=%fused_computation.30 | convolution fusion | flops 5640814592 | bytes 13238272 | tf_op jit(solution)/shard_map/transpose(jvp())/dot_general | solution.py:18
  60.9 23.2 %fusion.2 = (bf16[2048,1792]{1,0:T(8,128)(2,1)}, f32[2048,1792]{1,0:T(8,128)}) fusion(f32[2048,1792]{1,0:T(8,128)} %fusion.49, bf16[2048,1792]{1,0:T(8,128)(2,1)} %convolution_convert_fusion.1, bf16[2,768,1792]{2,1,0:T(8,128)(2,1)} %param.13, bf16[2048,768]{0,1:T(8,128)(2,1)} %copy-done.7, f32[2048]{0:T(1024)S(1)} %fusion.79), kind=kOutput, calls=%fused_computation.8 | convolution fusion | flops 5685903360 | bytes 49946624 | tf_op jit(solution)/shard_map/jvp()/dot_general | solution.py:29
  84.1 14.2 %fusion.40 = bf16[1,1792,768]{2,1,0:T(8,128)(2,1)} fusion(bf16[1,2048,768]{2,1,0:T(8,128)(2,1)S(1)} %copy-done.6, f32[2048,1792]{1,0:T(8,128)} %fusion.49, f32[2048,1792]{1,0:T(8,128)} %get-tuple-element.38), kind=kOutput, calls=%fused_computation.63 | convolution fusion | flops 5660540928 | bytes 35258368 | tf_op jit(solution)/shard_map/transpose(jvp())/dot_general | solution.py:18
  98.3 0.0 copy-start.8
  98.3 9.1 %convolution_convert_fusion.3 = bf16[2048,768]{0,1:T(8,128)(2,1)S(1)} fusion(bf16[2048,1792]{1,0:T(8,128)(2,1)} %get-tuple-element.37, bf16[2,768,1792]{2,1,0:T(8,128)(2,1)} %param.13), kind=kOutput, calls=%fused_computation.45 | convolution fusion | flops 5637144576 | bytes 13238272 | tf_op jit(solution)/shard_map/transpose(jvp())/dot_general | solution.py:29
  107.4 0.0 copy-done.8
  107.4 0.0 copy-start.13
  107.4 13.2 %fusion.21 = (f32[2048]{0:T(1024)S(1)}, bf16[2048,768]{0,1:T(8,128)(2,1)}) fusion(bf16[2048,768]{0,1:T(8,128)(2,1)S(1)} %copy-done.8, bf16[2048,768]{0,1:T(8,128)(2,1)S(1)} %convolution_convert_fusion.3, bf16[2,768,1792]{2,1,0:T(8,128)(2,1)} %param.14, bf16[2048,1792]{1,0:T(8,128)(2,1)} %convolution_convert_fusion.1, f32[2048,1792]{1,0:T(8,128)} %get-tuple-element.38), kind=kOutput, calls=%fused_computation.39 | convolution fusion | flops 5668599808 | bytes 34217984 | tf_op jit(solution)/shard_map/transpose(jvp())/dot_general | solution.py:30
  120.6 0.0 copy-done.13
  120.6 3.2 copy.21
  123.8 5.0 fusion.30
  128.9 0.0 copy-start.10
  128.9 8.9 %fusion.37 = bf16[1,1792,768]{2,1,0:T(8,128)(2,1)S(1)} fusion(bf16[2048,1792]{1,0:T(8,128)(2,1)} %get-tuple-element.33, bf16[2048,768]{0,1:T(8,128)(2,1)S(1)} %fusion.30), kind=kOutput, calls=%fused_computation.60 | convolution fusion | flops 5638520832 | bytes 13238272 | tf_op jit(solution)/shard_map/transpose(jvp())/dot_general | solution.py:18
  137.8 0.0 copy-done.10
  137.8 0.0 copy-start.9
  137.8 0.0 slice-start.4
  137.8 3.2 pad_add_fusion
  141.0 0.1 copy-done.9
  141.0 0.0 slice-start.5
  141.0 13.3 %fusion.39 = bf16[1,768,1792]{2,1,0:T(8,128)(2,1)} fusion(bf16[2048,1792]{1,0:T(8,128)(2,1)} %convolution_convert_fusion.1, bf16[2048,768]{0,1:T(8,128)(2,1)S(1)} %copy-done.9, f32[2048]{0:T(1024)S(1)} %fusion.79, f32[2048,1792]{1,0:T(8,128)} %get-tuple-element.38), kind=kOutput, calls=%fused_computation.62 | convolution fusion | flops 5665259520 | bytes 27926528 | tf_op jit(solution)/shard_map/transpose(jvp())/dot_general | solution.py:30
  154.3 0.0 slice-done.4
  154.3 0.0 slice-done.5
  154.3 0.0 copy-start.5
  154.3 0.0 copy-start.15
  154.3 8.0 %convolution_convert_fusion = bf16[2048,1792]{1,0:T(8,128)(2,1)} fusion(bf16[2048,768]{0,1:T(8,128)(2,1)S(1)} %fusion.30, bf16[2,1792,768]{2,1,0:T(8,128)(2,1)S(1)} %bitcast.96), kind=kOutput, calls=%fused_computation.29 | convolution fusion | flops 5640814592 | bytes 13238272 | tf_op jit(solution)/shard_map/transpose(jvp())/dot_general | solution.py:18
  162.4 0.0 copy-done.5
  162.4 0.0 copy-done.15
  162.4 11.7 %fusion.38 = bf16[1,768,1792]{2,1,0:T(8,128)(2,1)S(1)} fusion(bf16[2048,1792]{1,0:T(8,128)(2,1)} %convolution_convert_fusion, bf16[1,2048,768]{1,2,0:T(8,128)(2,1)S(1)} %copy-done.5, f32[2048]{0:T(1024)S(1)} %copy-done.15, f32[2048,1792]{1,0:T(8,128)} %fusion.56), kind=kOutput, calls=%fused_computation.61 | convolution fusion | flops 5665259520 | bytes 27926528 | tf_op jit(solution)/shard_map/transpose(jvp())/dot_general | solution.py:30
  174.1 0.0 copy-done.11
  174.1 2.8 pad_add_fusion.1
  176.9 10.3 %fusion.36 = bf16[1,768,1792]{2,1,0:T(8,128)(2,1)} fusion(bf16[2048,1792]{1,0:T(8,128)(2,1)} %get-tuple-element.37, bf16[2048,768]{0,1:T(8,128)(2,1)S(1)} %copy-done.9, f32[2048]{0:T(1024)S(1)} %fusion.79), kind=kOutput, calls=%fused_computation.59 | convolution fusion | flops 5641863168 | bytes 13246464 | tf_op jit(solution)/shard_map/transpose(jvp())/dot_general | solution.py:29
  187.2 16.8 %fusion.33 = bf16[1,768,1792]{2,1,0:T(8,128)(2,1)} fusion(f32[2048,1792]{1,0:T(8,128)} %fusion.56, f32[2048,1792]{1,0:T(8,128)} %get-tuple-element.34, bf16[2048,1792]{1,0:T(8,128)(2,1)} %convolution_convert_fusion, bf16[1,2048,768]{1,2,0:T(8,128)(2,1)S(1)} %copy-done.5, f32[2048]{0:T(1024)S(1)} %copy-done.15), kind=kOutput, calls=%fused_computation.58 | convolution fusion | flops 5683609600 | bytes 42606592 | tf_op jit(solution)/shard_map/transpose(jvp())/dot_general | solution.py:29
  204.0 0.0 copy-start.3
  204.0 5.6 %pad_add_fusion.2 = bf16[2,768,1792]{2,1,0:T(8,128)(2,1)} fusion(bf16[1,768,1792]{2,1,0:T(8,128)(2,1)} %fusion.33, bf16[1,768,1792]{2,1,0:T(8,128)(2,1)} %fusion.36), kind=kLoop, calls=%fused_computation.43 | loop fusion | flops 2752512 | bytes 11010048 | tf_op jit(solution)/shard_map/transpose(jvp())/add_any | solution.py:36
  209.5 0.0 copy-done
  209.5 0.0 copy-done.1
  209.5 0.0 copy-done.2
  209.6 0.0 copy-done.3
  209.6 332.4 %exchange.1 = (bf16[21,8,2,96,256]{4,3,2,1,0:T(8,128)(2,1)S(1)}, f32[21,2,96,256]{3,2,1,0:T(8,128)S(1)}, f32[21,2,96,256]{3,2,1,0:T(8,128)S(1)}) custom-call(bf16[2,8,96,1792]{3,2,1,0:T(8,128)(2,1)} %bitcast.87, bf16[2,8,96,1792]{3,2,1,0:T(8,128)(2,1)} %bitcast.86, bf16[2,8,224,768]{3,2,1,0:T(8,128)(2,1)} %bitcast.85, bf16[2,8,96,1792]{3,2,1,0:T(8,128)(2,1)} %bitcast.88, ...), custom_call_target="tpu_custom_call" | custom-call | tf_op jit(solution)/shard_map/exchange/pallas_call | solution.py:245
  541.9 8.2 %place.1 = (bf16[2,8,96,1792]{3,2,1,0:T(8,128)(2,1)}, bf16[2,8,96,1792]{3,2,1,0:T(8,128)(2,1)}, bf16[2,8,224,768]{3,2,1,0:T(8,128)(2,1)}, f32[2,96,1792]{2,1,0:T...) custom-call(bf16[21,8,2,96,256]{4,3,2,1,0:T(8,128)(2,1)S(1)} %get-tu, ...), custom_call_target="tpu_custom_call" | custom-call | tf_op jit(solution)/shard_map/place/pallas_call | solution.py:270
  (10 shorter events, 0.0 us)
Async XLA Ops:
  3.8 29.9 %copy-start.4 = (bf16[1,2048,768]{1,2,0:T(8,128)(2,1)}, bf16[1,2048,768]{1,2,0:T(8,128)(2,1)S(1)}, u32[]{:S(2)}) copy-start(bf16[1,2048,768]{1,2,0:T(8,128)(2,1)S(1)} %copy.20) | copy-start | bytes 9437188
  3.8 13.6 %slice-start = ((s8[5505024]{0:T(1024)(128)(4,1)}), s8[4194304]{0:T(1024)(128)(4,1)S(1)}, s32[]{:S(2)}) async-start(s8[5505024]{0:T(1024)(128)(4,1)} %bitcast.90), calls=%async_computation | async-start | bytes 8388608
  4.5 12.9 %copy-start.14 = (f32[2048]{0:T(1024)}, f32[2048]{0:T(1024)S(1)}, u32[]{:S(2)}) copy-start(f32[2048]{0:T(1024)S(1)} %add_rsqrt_fusion) | copy-start | bytes 24580
  4.5 12.9 %slice-start.1 = ((s8[5505024]{0:T(1024)(128)(4,1)}), s8[1310720]{0:T(1024)(128)(4,1)S(1)}, s32[]{:S(2)}) async-start(s8[5505024]{0:T(1024)(128)(4,1)} %bitcast.90), calls=%async_computation.1 | async-start | bytes 2621440
  33.8 19.0 %slice-start.2 = ((s8[5505024]{0:T(1024)(128)(4,1)}), s8[1310720]{0:T(1024)(128)(4,1)S(1)}, s32[]{:S(2)}) async-start(s8[5505024]{0:T(1024)(128)(4,1)} %bitcast.93), calls=%async_computation.2 | async-start | bytes 2621440
  43.3 9.4 %copy-start.7 = (bf16[2048,768]{0,1:T(8,128)(2,1)}, bf16[2048,768]{0,1:T(8,128)(2,1)S(1)}, u32[]{:S(2)}) copy-start(bf16[2048,768]{0,1:T(8,128)(2,1)S(1)} %get-tuple-element.36) | copy-start | bytes 9437188
  43.3 9.4 %copy-start.12 = (f32[2048]{0:T(1024)}, f32[2048]{0:T(1024)S(1)}, u32[]{:S(2)}) copy-start(f32[2048]{0:T(1024)S(1)} %get-tuple-element.35) | copy-start | bytes 24580
  43.3 9.4 %slice-start.3 = ((s8[5505024]{0:T(1024)(128)(4,1)}), s8[4194304]{0:T(1024)(128)(4,1)S(1)}, s32[]{:S(2)}) async-start(s8[5505024]{0:T(1024)(128)(4,1)} %bitcast.93), calls=%async_computation.3 | async-start | bytes 8388608
  43.3 9.4 %copy-start.6 = (bf16[1,2048,768]{2,1,0:T(8,128)(2,1)S(1)}, bf16[1,2048,768]{2,1,0:T(8,128)(2,1)}, u32[]{:S(2)}) copy-start(bf16[1,2048,768]{2,1,0:T(8,128)(2,1)} %param.12) | copy-start | bytes 9437188
  98.3 9.1 %copy-start.8 = (bf16[2048,768]{0,1:T(8,128)(2,1)S(1)}, bf16[2048,768]{0,1:T(8,128)(2,1)}, u32[]{:S(2)}) copy-start(bf16[2048,768]{0,1:T(8,128)(2,1)} %copy-done.7) | copy-start | bytes 9437188
  107.4 13.2 %copy-start.13 = (f32[2048]{0:T(1024)S(1)}, f32[2048]{0:T(1024)}, u32[]{:S(2)}) copy-start(f32[2048]{0:T(1024)} %copy-done.12) | copy-start | bytes 24580
  128.9 8.9 %copy-start.10 = (bf16[1,1792,768]{2,1,0:T(8,128)(2,1)S(1)}, bf16[1,1792,768]{2,1,0:T(8,128)(2,1)}, u32[]{:S(2)}) copy-start(bf16[1,1792,768]{2,1,0:T(8,128)(2,1)} %fusion.40) | copy-start | bytes 8257540
  137.8 3.3 copy-start.9
  137.8 16.5 %slice-start.4 = ((s8[5505024]{0:T(1024)(128)(4,1)}), s8[4194304]{0:T(1024)(128)(4,1)S(1)}, s32[]{:S(2)}) async-start(s8[5505024]{0:T(1024)(128)(4,1)} %bitcast.95), calls=%async_computation.4 | async-start | bytes 8388608
  141.0 13.3 %slice-start.5 = ((s8[5505024]{0:T(1024)(128)(4,1)}), s8[1310720]{0:T(1024)(128)(4,1)S(1)}, s32[]{:S(2)}) async-start(s8[5505024]{0:T(1024)(128)(4,1)} %bitcast.95), calls=%async_computation.5 | async-start | bytes 2621440
  154.3 8.1 %copy-start.5 = (bf16[1,2048,768]{1,2,0:T(8,128)(2,1)S(1)}, bf16[1,2048,768]{1,2,0:T(8,128)(2,1)}, u32[]{:S(2)}) copy-start(bf16[1,2048,768]{1,2,0:T(8,128)(2,1)} %copy-done.4) | copy-start | bytes 9437188
  154.3 8.1 %copy-start.15 = (f32[2048]{0:T(1024)S(1)}, f32[2048]{0:T(1024)}, u32[]{:S(2)}) copy-start(f32[2048]{0:T(1024)} %copy-done.14) | copy-start | bytes 24580
  162.4 11.7 %copy-start.11 = (bf16[1,768,1792]{2,1,0:T(8,128)(2,1)S(1)}, bf16[1,768,1792]{2,1,0:T(8,128)(2,1)}, u32[]{:S(2)}) copy-start(bf16[1,768,1792]{2,1,0:T(8,128)(2,1)} %fusion.39) | copy-start | bytes 8257540
  204.0 5.6 %copy-start = (f32[2,96,1792]{2,1,0:T(8,128)S(1)}, f32[2,96,1792]{2,1,0:T(8,128)}, u32[]{:S(2)}) copy-start(f32[2,96,1792]{2,1,0:T(8,128)} %refs_6_.1) | copy-start | bytes 4128772
  204.0 5.6 %copy-start.1 = (f32[2,96,1792]{2,1,0:T(8,128)S(1)}, f32[2,96,1792]{2,1,0:T(8,128)}, u32[]{:S(2)}) copy-start(f32[2,96,1792]{2,1,0:T(8,128)} %refs_7_.1) | copy-start | bytes 4128772
  204.0 5.6 %copy-start.2 = (f32[2,224,768]{2,1,0:T(8,128)S(1)}, f32[2,224,768]{2,1,0:T(8,128)}, u32[]{:S(2)}) copy-start(f32[2,224,768]{2,1,0:T(8,128)} %refs_8_.1) | copy-start | bytes 4128772
  204.0 5.6 %copy-start.3 = (f32[2,96,1792]{2,1,0:T(8,128)S(1)}, f32[2,96,1792]{2,1,0:T(8,128)}, u32[]{:S(2)}) copy-start(f32[2,96,1792]{2,1,0:T(8,128)} %refs_9_.1) | copy-start | bytes 4128772

commit v2 on v0

v2 whole, which is shorter than its diff:
```python
import jax
import jax.numpy as jnp
from jax import lax
from jax.experimental import pallas as pl
from jax.experimental.pallas import tpu as pltpu
from jax.sharding import PartitionSpec as P

MESH = pl.DeviceIdType.MESH
F32, BF16 = jnp.float32, jnp.bfloat16
COLS = 256
TILE = 512
VMEM = 67_043_328
EVERY = slice(None)


def dot(a, b, contract=(1, 0)):
    return lax.dot_general(a, b, (((contract[0],), (contract[1],)), ((), ())), preferred_element_type=F32)


def normed(h):
    wide = h.astype(F32)
    return (wide * lax.rsqrt(jnp.mean(wide * wide, -1, keepdims=True) + 1e-6)).astype(BF16)


def sigmoid(x):
    return 0.5 * jnp.tanh(0.5 * x) + 0.5


class Plan:
    def __init__(self, n, tokens, layers, d, ff):
        self.n, self.tokens, self.layers, self.d, self.ff = n, tokens, layers, d, ff
        self.rows, self.block = d // n, ff // n
        self.folds, self.chunks = d // COLS, ff // COLS
        self.strip = self.rows // self.folds
        self.strips = self.block // self.strip
        self.hops = n // 2
        assert layers == 2 and n % 2 == 0 and d % COLS == 0 and ff % COLS == 0 and tokens % TILE == 0
        assert self.rows % (16 * self.folds) == 0 and self.block % self.strip == 0 and COLS % self.strip == 0
        self.subs, late = [], []
        for l in reversed(range(layers)):
            for c in range(self.chunks):
                self.subs += [("gate", l, c), ("up", l, c)]
            late += [("down", l, s) for s in range(self.strips)]
            even = len(late) // 2 * 2
            self.subs, late = self.subs + late[:even], late[even:]
        assert not late
        self.units = len(self.subs) // 2
        self.at = {sub: i for i, sub in enumerate(self.subs)}

    def down_sub(self, l, s):
        first = self.at["down", l, 0]
        steps = [self.at["down", l, k] - self.at["down", l, k - 1] - 1 for k in range(1, self.strips)]
        place = first + s
        for k, extra in enumerate(steps, 1):
            if extra:
                place += lax.div(s + (self.strips - k), self.strips) * extra
        return place

    def views(self, i, own, arrays, lead=()):
        kind, l, k = self.subs[i]
        gate, up, down = arrays
        if kind != "down":
            yield own(i, pl.ds(0, self.rows)), (gate if kind == "gate" else up).at[(l, *lead, EVERY, pl.ds(k * COLS, COLS))]
        else:
            for f in range(self.folds):
                yield (
                    own(i, pl.ds(f * self.strip, self.strip)),
                    down.at[(l, *lead, pl.ds(k * self.strip, self.strip), pl.ds(f * COLS, COLS))],
                )


def flat(ref, rows, first=0):
    return lambda i, part: ref.at[pl.ds((first + i) * rows + part.start, part.size)]


def step_kernel(plan, count, x, dy, weights, blocks, moments_m, moments_v, own, mv, *scratch):
    (x_buf, a, dh, h1, sdd, gate_buf, up_buf, down_buf, half_landing, landing, squares, sums) = scratch[:12]
    (in_sems, weight_sems, state_sems, send, recv, tell_send, tell_recv) = scratch[12:]
    n, hops, units, chunks, rows, tokens = plan.n, plan.hops, plan.units, plan.chunks, plan.rows, plan.tokens
    me = lax.axis_index("dp")
    right, left = lax.rem(me + 1, n), lax.rem(me + n - 1, n)

    def at(k):
        return lax.rem(me + k + n, n)

    barrier = pltpu.get_barrier_semaphore()
    for k in range(1, n):
        pl.semaphore_signal(barrier, inc=1, device_id={"dp": at(k)}, device_id_type=MESH)

    s_, dg_, du_ = (sdd.at[pl.ds(i * tokens, tokens)] for i in range(3))
    acc = mv
    tiles = [pl.ds(t, TILE) for t in range(0, tokens, TILE)]

    def part(f, t):
        return pl.ds(f * tokens + t.start, TILE)

    passes = (0, 1, 0)

    def weight_copies(l, c, slot):
        chunk = pl.ds(pl.multiple_of(c * COLS, COLS), COLS)
        for i, (source, target) in enumerate(
            ((weights[0].at[l, :, chunk], gate_buf), (weights[1].at[l, :, chunk], up_buf), (weights[2].at[l, chunk], down_buf))
        ):
            yield pltpu.make_async_copy(source, target.at[slot], weight_sems.at[i, slot])

    def begin(k, c):
        slot = lax.rem(k * chunks + c, 2)
        for copy in weight_copies(passes[k], c, slot):
            copy.wait()

        @pl.when(c + 1 < chunks)
        def _():
            for copy in weight_copies(passes[k], c + 1, 1 - slot):
                copy.start()

        if k + 1 < len(passes):

            @pl.when(c + 1 == chunks)
            def _():
                for copy in weight_copies(passes[k + 1], 0, 1 - slot):
                    copy.start()

        return slot

    def add_to_acc(t, value):
        for f in range(plan.folds):
            acc[part(f, t)] += value[:, f * COLS : (f + 1) * COLS]

    def clear_acc():
        for f in range(plan.folds):
            acc[pl.ds(f * tokens, tokens)] = jnp.zeros((tokens, COLS), F32)

    def read_acc(t):
        return jnp.concatenate([acc[part(f, t)] for f in range(plan.folds)], axis=1).astype(BF16).astype(F32)

    load_x = pltpu.make_async_copy(x, x_buf, in_sems.at[0])
    load_dy = pltpu.make_async_copy(dy, dh, in_sems.at[1])
    load_x.start()
    for copy in weight_copies(0, 0, 0):
        copy.start()
    load_dy.start()
    load_x.wait()

    clear_acc()
    for t in tiles:
        a[t] = normed(x_buf[t])

    @pl.loop(0, chunks)
    def _(c):
        slot = begin(0, c)
        for t in tiles:
            gate, up = dot(a[t], gate_buf[slot]), dot(a[t], up_buf[slot])
            add_to_acc(t, dot((gate * sigmoid(gate) * up).astype(BF16), down_buf[slot]))

    for t in tiles:
        h = (x_buf[t].astype(F32) + read_acc(t)).astype(BF16)
        h1[t] = h
        a[t] = normed(h)
    clear_acc()
    load_dy.wait()

    def hop(p, h, d):
        b = at(hops - h) if d == 0 else at(h - hops)
        if h == 0:
            source, target = own.at[p, b, d], half_landing.at[p, d]
        else:
            source, target = own.at[p, b], landing.at[p, d, h - 1]
        return pltpu.make_async_remote_copy(
            source, target, send.at[p, h, d], recv.at[p, h, d], device_id={"dp": right if d == 0 else left}, device_id_type=MESH
        )

    def advance(p, h):
        for d in (0, 1):
            if h > 0:
                hop(p, h - 1, d).wait_recv()
                b = at(hops - h) if d == 0 else at(h - hops)
                if h == 1:
                    own[p, b, d] = (own[p, b, d].astype(F32) + half_landing[p, d].astype(F32)).astype(BF16)
                else:
                    own[p, b] = (own[p, b].astype(F32) + landing[p, d, h - 2].astype(F32)).astype(BF16)
            hop(p, h, d).start()

    def finish(p):
        for d in (0, 1):
            hop(p, hops - 1, d).wait_recv()
        for half in (0, 1):
            g = own[p, me, half].astype(F32) + landing[p, 0, hops - 2, half].astype(F32) + landing[p, 1, hops - 2, half].astype(F32)
            g = g.astype(BF16)
            own[p, me, half] = g
            g = g.astype(F32)
            squares[...] += g * g

    def serve(t):
        for h in range(hops):

            @pl.when(jnp.logical_and(t - h >= 0, t - h < units))
            def _(h=h):
                advance(t - h, h)

        @pl.when(jnp.logical_and(t - hops >= 0, t - hops < units))
        def _():
            finish(t - hops)

    def chunk_gradients(k, c, first, serve_now):
        l = passes[k]
        slot = begin(k, c)
        for t in tiles:
            gate, up = dot(a[t], gate_buf[slot]), dot(a[t], up_buf[slot])
            ds = dot(dh[t], down_buf[slot], (1, 1)).astype(BF16).astype(F32)
            sig = sigmoid(gate)
            silu = gate * sig
            s_[t] = (silu * up).astype(BF16)
            du_[t] = (ds * silu).astype(BF16)
            dg_[t] = (ds * up * (sig + silu * (1.0 - sig))).astype(BF16)
        for half, by in ((0, dg_), (1, du_)):
            own[first + c, :, half] = dot(a[...], by[...], (0, 0)).astype(BF16).reshape(n, rows, COLS)
        serve_now()
        by_down = dot(s_[...], dh[...], (0, 0)).astype(BF16)
        for g in range(COLS // plan.strip):
            group = c * (COLS // plan.strip) + g
            b, s = lax.div(group, plan.strips), lax.rem(group, plan.strips)
            i = plan.down_sub(l, s)
            for f in range(plan.folds):
                own[lax.div(i, 2), b, lax.rem(i, 2), f * plan.strip : (f + 1) * plan.strip] = by_down[
                    g * plan.strip : (g + 1) * plan.strip, f * COLS : (f + 1) * COLS
                ]
        return slot

    pl.semaphore_wait(barrier, n - 1)
    squares[...] = jnp.zeros_like(squares)

    @pl.loop(0, chunks)
    def _(c):
        slot = chunk_gradients(1, c, plan.at["gate", 1, 0] // 2, lambda: serve(c))
        for t in tiles:
            add_to_acc(t, dot(dg_[t], gate_buf[slot], (1, 1)) + dot(du_[t], up_buf[slot], (1, 1)))

    for t in tiles:
        h, da = h1[t].astype(F32), read_acc(t)
        scale = lax.rsqrt(jnp.mean(h * h, -1, keepdims=True) + 1e-6)
        by_norm = scale * da - h * (scale * scale * scale * jnp.mean(da * h, -1, keepdims=True))
        dh[t] = (dh[t].astype(F32) + by_norm.astype(BF16).astype(F32)).astype(BF16)
        a[t] = normed(x_buf[t])

    @pl.loop(0, chunks)
    def _(c):
        chunk_gradients(2, c, plan.at["gate", 0, 0] // 2, lambda: serve(chunks + c))

    w_block, m_block, v_block = flat(sdd, rows), flat(mv, rows), flat(mv, rows, len(plan.subs))
    held = len(plan.subs) * rows
    for s, (block, arrays) in enumerate(((w_block, [b.at[:, me] for b in blocks]), (m_block, moments_m), (v_block, moments_v))):
        for i in range(len(plan.subs)):
            for inside, outside in plan.views(i, block, arrays):
                pltpu.make_async_copy(outside, inside, state_sems.at[s]).start()

    @pl.loop(2 * chunks, units + hops)
    def _(t):
        serve(t)

    @pl.loop(0, units)
    def _(p):
        for h in range(hops):
            for d in (0, 1):
                hop(p, h, d).wait_send()

    folded = jnp.sum(squares[...].reshape(-1, 8, COLS), axis=0)
    sums[0] = sum(folded[:, i : i + 128] for i in range(0, COLS, 128))

    def tell(k):
        return pltpu.make_async_remote_copy(
            sums.at[0], sums.at[k], tell_send.at[k], tell_recv.at[k], device_id={"dp": at(k)}, device_id_type=MESH
        )

    for k in range(1, n):
        tell(k).start()
    for s, ref in enumerate((sdd.at[pl.ds(0, held)], mv.at[pl.ds(0, held)], mv.at[pl.ds(held, held)])):
        pltpu.make_async_copy(ref, ref, state_sems.at[s]).wait()
    for k in range(1, n):
        tell(k).wait_recv()
    total = jnp.sum(jnp.sum(sums[...], axis=0), axis=(0, 1), keepdims=True)
    factor = jnp.minimum(1.0, 0.5 * lax.rsqrt(total / count + 1e-30))
    for k in range(1, n):
        tell(k).wait_send()

    def pass_on(p, h, d):
        b = at(-h) if d == 0 else at(h)
        ref = own.at[p, b] if h < hops - 1 else own.at[p, b, d]
        return pltpu.make_async_remote_copy(
            ref, ref, send.at[p, h, d], recv.at[p, h, d], device_id={"dp": right if d == 0 else left}, device_id_type=MESH
        )

    @pl.loop(0, units)
    def _(p):
        for half in (0, 1):
            start = pl.multiple_of((2 * p + half) * rows, rows)
            here, there = pl.ds(start, rows), pl.ds(start + held, rows)
            g = own[p, me, half].astype(F32) * factor
            m = 0.9 * mv[here] + 0.1 * g
            v = 0.95 * mv[there] + 0.05 * g * g
            w = sdd[here].astype(F32)
            own[p, me, half] = (w - 0.02 * (m * lax.rsqrt(v + 1e-8) + 0.1 * w)).astype(BF16)
            mv[here] = m
            mv[there] = v
        for d in (0, 1):
            pass_on(p, 0, d).start()

    for h in range(1, hops):

        @pl.loop(0, units)
        def _(p, h=h):
            for d in (0, 1):
                pass_on(p, h - 1, d).wait_recv()
                pass_on(p, h, d).start()

    @pl.loop(0, units)
    def _(p):
        for d in (0, 1):
            pass_on(p, hops - 1, d).wait_recv()
            for h in range(hops):
                pass_on(p, h, d).wait_send()


def place_kernel(plan, own, mv, weights, new_m, new_v, sems):
    def gathered(i, part):
        return own.at[i // 2, :, i % 2, part]

    copies = []
    for i in range(len(plan.subs)):
        for s, (block, arrays, lead) in enumerate(
            (
                (gathered, weights, (EVERY,)),
                (flat(mv, plan.rows), new_m, ()),
                (flat(mv, plan.rows, len(plan.subs)), new_v, ()),
            )
        ):
            copies += [pltpu.make_async_copy(*views, sems.at[s]) for views in plan.views(i, block, arrays, lead)]
    for copy in copies:
        copy.start()
    for copy in copies:
        copy.wait()


def solution(mesh):
    n = mesh.shape["dp"]

    def step(x, dy, *arrays):
        weights, m, v = (arrays[i : i + 3] for i in (0, 3, 6))
        layers, d, ff = weights[0].shape
        tokens = x.shape[1]
        plan = Plan(n, tokens, layers, d, ff)
        blocks = [w.reshape(layers, n, -1, w.shape[-1]) for w in weights]
        count = float(sum(w.size for w in weights))
        units, rows, hops, subs = plan.units, plan.rows, plan.hops, len(plan.subs)
        anywhere, in_vmem = pl.BlockSpec(memory_space=pl.ANY), pl.BlockSpec(memory_space=pltpu.VMEM)

        def body(x, dy, *refs):
            weights, blocks, m, v = (refs[i : i + 3] for i in (0, 3, 6, 9))
            step_kernel(plan, count, x, dy, weights, blocks, m, v, *refs[12:])

        results = [pltpu.VMEM((units, n, 2, rows, COLS), BF16), pltpu.VMEM((2 * subs * rows, COLS), F32)]
        own, mv = pl.pallas_call(
            body,
            out_shape=results,
            in_specs=[anywhere] * 14,
            out_specs=[in_vmem] * 2,
            scratch_shapes=[pltpu.VMEM((tokens, d), BF16)] * 4
            + [
                pltpu.VMEM((3 * tokens, COLS), BF16),
                pltpu.VMEM((2, d, COLS), BF16),
                pltpu.VMEM((2, d, COLS), BF16),
                pltpu.VMEM((2, COLS, d), BF16),
                pltpu.VMEM((units, 2, rows, COLS), BF16),
                pltpu.VMEM((units, 2, hops - 1, 2, rows, COLS), BF16),
                pltpu.VMEM((rows, COLS), F32),
                pltpu.VMEM((n, 8, 128), F32),
                pltpu.SemaphoreType.DMA((2,)),
                pltpu.SemaphoreType.DMA((3, 2)),
                pltpu.SemaphoreType.DMA((3,)),
                pltpu.SemaphoreType.DMA((units, hops, 2)),
                pltpu.SemaphoreType.DMA((units, hops, 2)),
                pltpu.SemaphoreType.DMA((n,)),
                pltpu.SemaphoreType.DMA((n,)),
            ],
            compiler_params=pltpu.CompilerParams(collective_id=0, has_side_effects=True, vmem_limit_bytes=38 * 2**20),
            name="step",
        )(x[0], dy[0], *weights, *blocks, *m, *v)

        def place(*refs):
            place_kernel(plan, *refs[:2], refs[2:5], refs[5:8], refs[8:11], refs[11])

        out = pl.pallas_call(
            place,
            out_shape=[jax.ShapeDtypeStruct(t.shape, t.dtype) for t in (*blocks, *m, *v)],
            in_specs=[in_vmem] * 2,
            out_specs=[anywhere] * 9,
            scratch_shapes=[pltpu.SemaphoreType.DMA((3,))],
            compiler_params=pltpu.CompilerParams(vmem_limit_bytes=2**20),
            name="place",
        )(own, mv)
        return tuple(o.reshape(w.shape) for o, w in zip(out[:3], weights)) + tuple(out[3:])

    block = P(None, "dp", None)
    sequence = P(("rep", "dp"), None, None)
    return jax.shard_map(
        step,
        mesh=mesh,
        in_specs=(sequence, sequence, P(), P(), P()) + (block,) * 6,
        out_specs=(P("rep"),) * 3 + (P("rep", "dp", None),) * 6,
        check_vma=False,
    )
```

time: 785 us -> 386 us (0.49); the launches traced: 775 us -> 386 us
  waiting for transfers between devices: 487 us -> 0 us
  Pallas kernels: 0 us -> 385 us
  matrix products: 171 us -> 0 us
  other arithmetic: 50.1 us -> 0 us
  local copies, waits for them, and re-layouts: 32.4 us -> 0 us
  between operations: 17.9 us -> 0.81 us
  blocking collectives: 16.7 us -> 0 us
    pallas_call x0 -> x2, Pallas kernels: none -> 385 us  [the longest x1 377 us: step(): pl.pallas_call(body, out_shape=results, in_specs=[anywhere] * 14, out_spe...]
    unnamed x15 -> x0, waiting for transfers between devices: 303 us -> none
    reshape x3 -> x0, waiting for transfers between devices: 184 us -> none  [step(): t.reshape(-1, *t.shape[2:])]
    dot_general x15 -> x0, matrix products: 171 us -> none  [the longest x5 63.1 us: layer(): up = jnp.dot(a, w['w_up'], preferred_element_type=jnp.float32)]
    unnamed x49 -> x0, local copies, waits for them, and re-layouts: 31.8 us -> none
    unnamed x5 -> x0, other arithmetic: 25 us -> none
    reduce_sum x1 -> x0, blocking collectives: 16.7 us -> none  [of_a_group(): jnp.sum(g * g)]
    reshape x3 -> x0, other arithmetic: 12.7 us -> none  [step(): t.reshape(-1, *t.shape[2:])]
  transfers between devices with their start and end apart: 9 -> 0, of which waited for: 8 -> 0; matrix products, arithmetic and copies ran while one was open for 12% -> 0% of each run, Pallas kernels for 0% -> 0%
where the time goes in v2:
time: 386 us
  Pallas kernels  385 us (100%)
    pallas_call x1, Pallas kernels, step(): pl.pallas_call(body, out_shape=results, in_specs=[anywhere] * 14, out_spe...  377 us
    pallas_call x1, Pallas kernels, step(): pl.pallas_call(place, out_shape=[jax.ShapeDtypeStruct(t.shape, t.dtype) f...  8.15 us

profile of v2, /device:TPU:28, one launch (start us, length us, event | category | flops | bytes accessed | tf_op | source)
XLA Modules:
  0.0 385.8 jit_solution(11442803053225172619)
XLA Ops:
  0.6 376.8 %step.1 = (bf16[21,8,2,96,256]{4,3,2,1,0:T(8,128)(2,1)S(1)}, f32[8064,256]{1,0:T(8,128)S(1)}) custom-call(bf16[2048,768]{1,0:T(8,128)(2,1)} %bitcast.11, bf16[2048,768]{1,0:T(8,128)(2,1)} %bitcast.12, bf16[2,768,1792]{2,1,0:T(8,128)(2,1)} %refs_0_.1, bf16[2,768,1792]{2,1,0:T(8,128)(2,1)} %refs_1_.1, bf16[2,1792,768]{2,1,0:T(8,128)(2,1)} %refs_2_.1, ...), custom_call_target="tpu_custom_call" | custom-call | tf_op jit(solution)/shard_map/step/pallas_call | solution.py:361
  377.5 8.2 %place.1 = (bf16[2,8,96,1792]{3,2,1,0:T(8,128)(2,1)}, bf16[2,8,96,1792]{3,2,1,0:T(8,128)(2,1)}, bf16[2,8,224,768]{3,2,1,0:T(8,128)(2,1)}, f32[2,96,1792]{2,1,0:T...) custom-call(bf16[21,8,2,96,256]{4,3,2,1,0:T(8,128)(2,1)S(1)} %get-tu, ...), custom_call_target="tpu_custom_call" | custom-call | tf_op jit(solution)/shard_map/place/pallas_call | solution.py:391

commit v3 on v2

--- a/solution.py
+++ b/solution.py
@@ -11,6 +11,14 @@
 TILE = 512
 VMEM = 67_043_328
 EVERY = slice(None)
+LATE = 99
+HOPS = (
+    (2, 5, 7, 11, 13, 16, 20, 20, 20, 21, 32, 34, 36, 39, 42, 46, *(LATE,) * 5),
+    (3, 6, 10, 13, 15, 19, 23, 24, 25, 25, 34, 35, 38, 42, 44, 48, *(LATE,) * 5),
+    (6, 8, 12, 16, 17, 21, 27, 27, 29, 33, 36, 38, 40, 44, 46, *(LATE,) * 6),
+    (9, 11, 15, 22, 24, 28, 29, 31, 31, 37, 40, 43, 45, 46, 49, *(LATE,) * 6),
+    (13, 15, 19, 26, 28, 32, 33, 35, 35, 41, 44, 47, 49, *(LATE,) * 8),
+)
 
 
 def dot(a, b, contract=(1, 0)):
@@ -45,6 +53,7 @@
             self.subs, late = self.subs + late[:even], late[even:]
         assert not late
         self.units = len(self.subs) // 2
+        assert self.hops + 1 == len(HOPS) and all(len(h) == self.units for h in HOPS)
         self.at = {sub: i for i, sub in enumerate(self.subs)}
 
     def down_sub(self, l, s):
@@ -73,9 +82,9 @@
     return lambda i, part: ref.at[pl.ds((first + i) * rows + part.start, part.size)]
 
 
-def step_kernel(plan, count, x, dy, weights, blocks, moments_m, moments_v, own, mv, *scratch):
-    (x_buf, a, dh, h1, sdd, gate_buf, up_buf, down_buf, half_landing, landing, squares, sums) = scratch[:12]
-    (in_sems, weight_sems, state_sems, send, recv, tell_send, tell_recv) = scratch[12:]
+def step_kernel(plan, count, x, dy, weights, blocks, moments_m, moments_v, own, mv, stash, *scratch):
+    (x_buf, a, dh, sdd, gate_buf, up_buf, down_buf, half_landing, landing, squares, sums) = scratch[:11]
+    (in_sems, weight_sems, stash_sems, state_sems, send, recv, tell_send, tell_recv) = scratch[11:]
     n, hops, units, chunks, rows, tokens = plan.n, plan.hops, plan.units, plan.chunks, plan.rows, plan.tokens
     me = lax.axis_index("dp")
     right, left = lax.rem(me + 1, n), lax.rem(me + n - 1, n)
@@ -87,17 +96,21 @@
     for k in range(1, n):
         pl.semaphore_signal(barrier, inc=1, device_id={"dp": at(k)}, device_id_type=MESH)
 
-    s_, dg_, du_ = (sdd.at[pl.ds(i * tokens, tokens)] for i in range(3))
+    s_, dg_, du_ = (sdd.at[pl.ds(i * tokens, tokens)] for i in (0, 2, 3))
+    pairs = [sdd.at[pl.ds(i * tokens, 2 * tokens)] for i in (2, 0)]
     acc = mv
     tiles = [pl.ds(t, TILE) for t in range(0, tokens, TILE)]
 
     def part(f, t):
         return pl.ds(f * tokens + t.start, TILE)
 
-    passes = (0, 1, 0)
+    passes = (0, 1, 1, 0)
+
+    def chunk_of(k, c):
+        return chunks - 1 - c if k == 2 else c
 
     def weight_copies(l, c, slot):
-        chunk = pl.ds(pl.multiple_of(c * COLS, COLS), COLS)
+        chunk = pl.ds(c * COLS if isinstance(c, int) else pl.multiple_of(c * COLS, COLS), COLS)
         for i, (source, target) in enumerate(
             ((weights[0].at[l, :, chunk], gate_buf), (weights[1].at[l, :, chunk], up_buf), (weights[2].at[l, chunk], down_buf))
         ):
@@ -105,19 +118,19 @@
 
     def begin(k, c):
         slot = lax.rem(k * chunks + c, 2)
-        for copy in weight_copies(passes[k], c, slot):
+        for copy in weight_copies(passes[k], chunk_of(k, c), slot):
             copy.wait()
 
         @pl.when(c + 1 < chunks)
         def _():
-            for copy in weight_copies(passes[k], c + 1, 1 - slot):
+            for copy in weight_copies(passes[k], chunk_of(k, c + 1), 1 - slot):
                 copy.start()
 
         if k + 1 < len(passes):
 
             @pl.when(c + 1 == chunks)
             def _():
-                for copy in weight_copies(passes[k + 1], 0, 1 - slot):
+                for copy in weight_copies(passes[k + 1], chunk_of(k + 1, 0), 1 - slot):
                     copy.start()
 
         return slot
@@ -126,37 +139,40 @@
         for f in range(plan.folds):
             acc[part(f, t)] += value[:, f * COLS : (f + 1) * COLS]
 
-    def clear_acc():
+    def read_acc(t):
+        return jnp.concatenate([acc[part(f, t)] for f in range(plan.folds)], axis=1)
+
+    loads = [pltpu.make_async_copy(x.at[t], x_buf.at[t], in_sems.at[i]) for i, t in enumerate(tiles)]
+    load_dy = pltpu.make_async_copy(dy, dh, in_sems.at[len(tiles)])
+    for copy in (*loads, *weight_copies(0, 0, 0), load_dy):
+        copy.start()
+
+    def forward(slot, t):
+        gate, up = dot(a[t], gate_buf[slot]), dot(a[t], up_buf[slot])
+        return dot((gate * sigmoid(gate) * up).astype(BF16), down_buf[slot])
+
+    slot = begin(0, 0)
+    for t, load in zip(tiles, loads):
+        load.wait()
+        a[t] = normed(x_buf[t])
+        value = forward(slot, t)
         for f in range(plan.folds):
-            acc[pl.ds(f * tokens, tokens)] = jnp.zeros((tokens, COLS), F32)
-
-    def read_acc(t):
-        return jnp.concatenate([acc[part(f, t)] for f in range(plan.folds)], axis=1).astype(BF16).astype(F32)
-
-    load_x = pltpu.make_async_copy(x, x_buf, in_sems.at[0])
-    load_dy = pltpu.make_async_copy(dy, dh, in_sems.at[1])
-    load_x.start()
-    for copy in weight_copies(0, 0, 0):
-        copy.start()
-    load_dy.start()
-    load_x.wait()
-
-    clear_acc()
-    for t in tiles:
-        a[t] = normed(x_buf[t])
-
-    @pl.loop(0, chunks)
+            acc[part(f, t)] = value[:, f * COLS : (f + 1) * COLS]
+
+    @pl.loop(1, chunks - 1)
     def _(c):
         slot = begin(0, c)
         for t in tiles:
-            gate, up = dot(a[t], gate_buf[slot]), dot(a[t], up_buf[slot])
-            add_to_acc(t, dot((gate * sigmoid(gate) * up).astype(BF16), down_buf[slot]))
-
+            add_to_acc(t, forward(slot, t))
+
+    slot = begin(0, chunks - 1)
     for t in tiles:
-        h = (x_buf[t].astype(F32) + read_acc(t)).astype(BF16)
-        h1[t] = h
+        add = read_acc(t) + forward(slot, t)
+        h = (x_buf[t].astype(F32) + add.astype(BF16).astype(F32)).astype(BF16)
+        for f in range(plan.folds):
+            acc[part(f, t)] = jnp.zeros((TILE, COLS), F32)
+        x_buf[t] = h
         a[t] = normed(h)
-    clear_acc()
     load_dy.wait()
 
     def hop(p, h, d):
@@ -190,20 +206,43 @@
             g = g.astype(F32)
             squares[...] += g * g
 
-    def serve(t):
-        for h in range(hops):
-
-            @pl.when(jnp.logical_and(t - h >= 0, t - h < units))
-            def _(h=h):
-                advance(t - h, h)
-
-        @pl.when(jnp.logical_and(t - hops >= 0, t - hops < units))
-        def _():
-            finish(t - hops)
-
-    def chunk_gradients(k, c, first, serve_now):
+    def serve(first, last, k):
+        for h in range(hops + 1):
+            before = sum(at < first for at in HOPS[h])
+            here = [at for at in HOPS[h] if first <= at <= last]
+            if not here:
+                continue
+            k = jnp.int32(k)
+            done = before + sum((k > at).astype(jnp.int32) for at in here)
+            now = sum((k == at).astype(jnp.int32) for at in here)
+
+            @pl.loop(done, done + now)
+            def _(p, h=h):
+                if h < hops:
+                    advance(p, h)
+                else:
+                    finish(p)
+
+    def serve_late():
+        first = [sum(at < LATE for at in places) for places in HOPS]
+        for h in range(hops + 1):
+
+            @pl.loop(first[h], units)
+            def _(p, h=h):
+                if h < hops:
+                    advance(p, h)
+                else:
+                    finish(p)
+
+    def chunk_gradients(k, c, first, places):
         l = passes[k]
         slot = begin(k, c)
+        if k == 1:
+
+            @pl.when(c > 0)
+            def _():
+                store(c - 1).wait()
+
         for t in tiles:
             gate, up = dot(a[t], gate_buf[slot]), dot(a[t], up_buf[slot])
             ds = dot(dh[t], down_buf[slot], (1, 1)).astype(BF16).astype(F32)
@@ -212,9 +251,16 @@
             s_[t] = (silu * up).astype(BF16)
             du_[t] = (ds * silu).astype(BF16)
             dg_[t] = (ds * up * (sig + silu * (1.0 - sig))).astype(BF16)
+        if k == 1:
+
+            @pl.when(c + 1 < chunks)
+            def _():
+                store(c).start()
+
+        serve(*places, places[0] + 3 * c)
         for half, by in ((0, dg_), (1, du_)):
             own[first + c, :, half] = dot(a[...], by[...], (0, 0)).astype(BF16).reshape(n, rows, COLS)
-        serve_now()
+        serve(*places, places[0] + 3 * c + 1)
         by_down = dot(s_[...], dh[...], (0, 0)).astype(BF16)
         for g in range(COLS // plan.strip):
             group = c * (COLS // plan.strip) + g
@@ -224,27 +270,63 @@
                 own[lax.div(i, 2), b, lax.rem(i, 2), f * plan.strip : (f + 1) * plan.strip] = by_down[
                     g * plan.strip : (g + 1) * plan.strip, f * COLS : (f + 1) * COLS
                 ]
-        return slot
+        serve(*places, places[0] + 3 * c + 2)
 
     pl.semaphore_wait(barrier, n - 1)
     squares[...] = jnp.zeros_like(squares)
 
+    def store(c):
+        return pltpu.make_async_copy(pairs[0], stash.at[c], stash_sems.at[2])
+
+    def fetch(c, pair):
+        return pltpu.make_async_copy(stash.at[chunk_of(2, c)], pairs[pair], stash_sems.at[pair])
+
+    places_1 = (0, 3 * chunks - 1)
+    places_in = (3 * chunks, 4 * chunks - 1)
+    place_norm = 4 * chunks
+    places_0 = (place_norm + 1, place_norm + 3 * chunks)
+
     @pl.loop(0, chunks)
     def _(c):
-        slot = chunk_gradients(1, c, plan.at["gate", 1, 0] // 2, lambda: serve(c))
-        for t in tiles:
-            add_to_acc(t, dot(dg_[t], gate_buf[slot], (1, 1)) + dot(du_[t], up_buf[slot], (1, 1)))
-
+        chunk_gradients(1, c, plan.at["gate", 1, 0] // 2, places_1)
+
+    @pl.loop(0, chunks)
+    def _(c):
+        slot = begin(2, c)
+
+        def add(pair):
+            @pl.when(c > 0)
+            def _():
+                fetch(c, pair).wait()
+
+            @pl.when(c + 1 < chunks)
+            def _():
+                fetch(c + 1, 1 - pair).start()
+
+            by_gate, by_up = (pairs[pair].at[pl.ds(i * tokens, tokens)] for i in (0, 1))
+            for t in tiles:
+                add_to_acc(t, dot(by_gate[t], gate_buf[slot], (1, 1)) + dot(by_up[t], up_buf[slot], (1, 1)))
+
+        for pair in (0, 1):
+            pl.when(lax.rem(c, 2) == pair)(lambda pair=pair: add(pair))
+        serve(*places_in, places_in[0] + c)
+
+    again = pltpu.make_async_copy(x, a, in_sems.at[0])
+    again.start()
     for t in tiles:
-        h, da = h1[t].astype(F32), read_acc(t)
+        h, da = x_buf[t].astype(F32), read_acc(t).astype(BF16).astype(F32)
         scale = lax.rsqrt(jnp.mean(h * h, -1, keepdims=True) + 1e-6)
         by_norm = scale * da - h * (scale * scale * scale * jnp.mean(da * h, -1, keepdims=True))
         dh[t] = (dh[t].astype(F32) + by_norm.astype(BF16).astype(F32)).astype(BF16)
-        a[t] = normed(x_buf[t])
+    again.wait()
+    for t in tiles:
+        a[t] = normed(a[t])
+
+    serve(place_norm, place_norm, place_norm)
 
     @pl.loop(0, chunks)
     def _(c):
-        chunk_gradients(2, c, plan.at["gate", 0, 0] // 2, lambda: serve(chunks + c))
+        chunk_gradients(3, c, plan.at["gate", 0, 0] // 2, places_0)
 
     w_block, m_block, v_block = flat(sdd, rows), flat(mv, rows), flat(mv, rows, len(plan.subs))
     held = len(plan.subs) * rows
@@ -253,9 +335,7 @@
             for inside, outside in plan.views(i, block, arrays):
                 pltpu.make_async_copy(outside, inside, state_sems.at[s]).start()
 
-    @pl.loop(2 * chunks, units + hops)
-    def _(t):
-        serve(t)
+    serve_late()
 
     @pl.loop(0, units)
     def _(p):
@@ -358,14 +438,15 @@
             step_kernel(plan, count, x, dy, weights, blocks, m, v, *refs[12:])
 
         results = [pltpu.VMEM((units, n, 2, rows, COLS), BF16), pltpu.VMEM((2 * subs * rows, COLS), F32)]
-        own, mv = pl.pallas_call(
+        results += [jax.ShapeDtypeStruct((plan.chunks, 2 * tokens, COLS), BF16)]
+        own, mv, _ = pl.pallas_call(
             body,
             out_shape=results,
             in_specs=[anywhere] * 14,
-            out_specs=[in_vmem] * 2,
-            scratch_shapes=[pltpu.VMEM((tokens, d), BF16)] * 4
+            out_specs=[in_vmem] * 2 + [anywhere],
+            scratch_shapes=[pltpu.VMEM((tokens, d), BF16)] * 3
             + [
-                pltpu.VMEM((3 * tokens, COLS), BF16),
+                pltpu.VMEM((4 * tokens, COLS), BF16),
                 pltpu.VMEM((2, d, COLS), BF16),
                 pltpu.VMEM((2, d, COLS), BF16),
                 pltpu.VMEM((2, COLS, d), BF16),
@@ -373,8 +454,9 @@
                 pltpu.VMEM((units, 2, hops - 1, 2, rows, COLS), BF16),
                 pltpu.VMEM((rows, COLS), F32),
                 pltpu.VMEM((n, 8, 128), F32),
-                pltpu.SemaphoreType.DMA((2,)),
+                pltpu.SemaphoreType.DMA((tokens // TILE + 1,)),
                 pltpu.SemaphoreType.DMA((3, 2)),
+                pltpu.SemaphoreType.DMA((3,)),
                 pltpu.SemaphoreType.DMA((3,)),
                 pltpu.SemaphoreType.DMA((units, hops, 2)),
                 pltpu.SemaphoreType.DMA((units, hops, 2)),

time: 386 us -> 370 us (0.959)
  Pallas kernels: 385 us -> 369 us
    pallas_call x1, Pallas kernels: 377 us -> 361 us  [step(): pl.pallas_call(body, out_shape=results, in_specs=[anywhere] * 14, out_spe...]
where the time goes in v3:
time: 370 us
  Pallas kernels  369 us (100%)
    pallas_call x1, Pallas kernels, step(): pl.pallas_call(body, out_shape=results, in_specs=[anywhere] * 14, out_spe...  361 us
    pallas_call x1, Pallas kernels, step(): pl.pallas_call(place, out_shape=[jax.ShapeDtypeStruct(t.shape, t.dtype) f...  8.15 us

profile of v3, /device:TPU:28, one launch (start us, length us, event | category | flops | bytes accessed | tf_op | source)
XLA Modules:
  0.0 369.6 jit_solution(9520147529437639229)
XLA Ops:
  0.6 360.6 %step.1 = (bf16[21,8,2,96,256]{4,3,2,1,0:T(8,128)(2,1)S(1)}, f32[8064,256]{1,0:T(8,128)S(1)}, bf16[7,4096,256]{2,1,0:T(8,128)(2,1)}) custom-call(bf16[2048,768]{1,0:T(8,128)(2,1)} %bitcast.11, bf16[2048,768]{1,0:T(8,128)(2,1)} %bitcast.12, bf16[2,768,1792]{2,1,0:T(8,128)(2,1)} %refs_0_.1, bf16[2,768,1792]{2,1,0:T(8,128)(2,1)} %refs_1_.1, ...), custom_call_target="tpu_custom_call" | custom-call | tf_op jit(solution)/shard_map/step/pallas_call | solution.py:442
  361.3 8.2 %place.1 = (bf16[2,8,96,1792]{3,2,1,0:T(8,128)(2,1)}, bf16[2,8,96,1792]{3,2,1,0:T(8,128)(2,1)}, bf16[2,8,224,768]{3,2,1,0:T(8,128)(2,1)}, f32[2,96,1792]{2,1,0:T...) custom-call(bf16[21,8,2,96,256]{4,3,2,1,0:T(8,128)(2,1)S(1)} %get-tu, ...), custom_call_target="tpu_custom_call" | custom-call | tf_op jit(solution)/shard_map/place/pallas_call | solution.py:473

commit v4 on v3

--- a/solution.py
+++ b/solution.py
@@ -13,11 +13,11 @@
 EVERY = slice(None)
 LATE = 99
 HOPS = (
-    (2, 5, 7, 11, 13, 16, 20, 20, 20, 21, 32, 34, 36, 39, 42, 46, *(LATE,) * 5),
-    (3, 6, 10, 13, 15, 19, 23, 24, 25, 25, 34, 35, 38, 42, 44, 48, *(LATE,) * 5),
-    (6, 8, 12, 16, 17, 21, 27, 27, 29, 33, 36, 38, 40, 44, 46, *(LATE,) * 6),
-    (9, 11, 15, 22, 24, 28, 29, 31, 31, 37, 40, 43, 45, 46, 49, *(LATE,) * 6),
-    (13, 15, 19, 26, 28, 32, 33, 35, 35, 41, 44, 47, 49, *(LATE,) * 8),
+    (1, 3, 5, 7, 10, 11, 13, 20, 20, 20, 23, 26, 30, 34, 36, 38, 42, 42, *(LATE,) * 3),
+    (3, 4, 7, 9, 12, 14, 15, 21, 21, 22, 27, 30, 32, 38, 38, 42, *(LATE,) * 5),
+    (5, 6, 11, 12, 14, 16, 18, 23, 24, 25, 31, 34, 37, 40, 40, *(LATE,) * 6),
+    (8, 9, 15, 17, 18, 19, 20, 28, 28, 30, 36, 37, 39, 42, *(LATE,) * 7),
+    (12, 13, 19, 21, 22, 23, 24, 32, 32, 34, 40, 41, *(LATE,) * 9),
 )
 
 
@@ -96,8 +96,10 @@
     for k in range(1, n):
         pl.semaphore_signal(barrier, inc=1, device_id={"dp": at(k)}, device_id_type=MESH)
 
-    s_, dg_, du_ = (sdd.at[pl.ds(i * tokens, tokens)] for i in (0, 2, 3))
-    pairs = [sdd.at[pl.ds(i * tokens, 2 * tokens)] for i in (2, 0)]
+    def held(slot, i, t=None):
+        start, size = (0, tokens) if t is None else (t.start, t.size)
+        return sdd.at[slot, pl.ds(i * tokens + start, size)]
+
     acc = mv
     tiles = [pl.ds(t, TILE) for t in range(0, tokens, TILE)]
 
@@ -144,35 +146,39 @@
 
     loads = [pltpu.make_async_copy(x.at[t], x_buf.at[t], in_sems.at[i]) for i, t in enumerate(tiles)]
     load_dy = pltpu.make_async_copy(dy, dh, in_sems.at[len(tiles)])
-    for copy in (*loads, *weight_copies(0, 0, 0), load_dy):
+    for copy in (loads[0], *weight_copies(0, 0, 0), *loads[1:]):
         copy.start()
 
-    def forward(slot, t):
-        gate, up = dot(a[t], gate_buf[slot]), dot(a[t], up_buf[slot])
-        return dot((gate * sigmoid(gate) * up).astype(BF16), down_buf[slot])
-
-    slot = begin(0, 0)
+    for f in range(plan.folds):
+        acc[pl.ds(f * tokens, tokens)] = jnp.zeros((tokens, COLS), F32)
     for t, load in zip(tiles, loads):
         load.wait()
         a[t] = normed(x_buf[t])
-        value = forward(slot, t)
-        for f in range(plan.folds):
-            acc[part(f, t)] = value[:, f * COLS : (f + 1) * COLS]
-
-    @pl.loop(1, chunks - 1)
-    def _(c):
+    load_dy.start()
+
+    def forward(c, use):
         slot = begin(0, c)
-        for t in tiles:
-            add_to_acc(t, forward(slot, t))
-
-    slot = begin(0, chunks - 1)
-    for t in tiles:
-        add = read_acc(t) + forward(slot, t)
-        h = (x_buf[t].astype(F32) + add.astype(BF16).astype(F32)).astype(BF16)
+        ready = None
+        for t in (*tiles, None):
+            if t is not None:
+                gate, up = dot(a[t], gate_buf[slot]), dot(a[t], up_buf[slot])
+                after = t, (gate * sigmoid(gate) * up).astype(BF16)
+            if ready is not None:
+                use(ready[0], dot(ready[1], down_buf[slot]))
+            ready = after
+
+    def next_input(t, value):
+        h = (x_buf[t].astype(F32) + (read_acc(t) + value).astype(BF16).astype(F32)).astype(BF16)
         for f in range(plan.folds):
             acc[part(f, t)] = jnp.zeros((TILE, COLS), F32)
         x_buf[t] = h
         a[t] = normed(h)
+
+    @pl.loop(0, chunks - 1)
+    def _(c):
+        forward(c, add_to_acc)
+
+    forward(chunks - 1, next_input)
     load_dy.wait()
 
     def hop(p, h, d):
@@ -205,6 +211,9 @@
             own[p, me, half] = g
             g = g.astype(F32)
             squares[...] += g * g
+        for h in range(hops):
+            for d in (0, 1):
+                hop(p, h, d).wait_send()
 
     def serve(first, last, k):
         for h in range(hops + 1):
@@ -234,34 +243,22 @@
                 else:
                     finish(p)
 
-    def chunk_gradients(k, c, first, places):
-        l = passes[k]
-        slot = begin(k, c)
-        if k == 1:
-
-            @pl.when(c > 0)
-            def _():
-                store(c - 1).wait()
-
+    def hidden(slot, h):
         for t in tiles:
             gate, up = dot(a[t], gate_buf[slot]), dot(a[t], up_buf[slot])
             ds = dot(dh[t], down_buf[slot], (1, 1)).astype(BF16).astype(F32)
             sig = sigmoid(gate)
             silu = gate * sig
-            s_[t] = (silu * up).astype(BF16)
-            du_[t] = (ds * silu).astype(BF16)
-            dg_[t] = (ds * up * (sig + silu * (1.0 - sig))).astype(BF16)
-        if k == 1:
-
-            @pl.when(c + 1 < chunks)
-            def _():
-                store(c).start()
-
-        serve(*places, places[0] + 3 * c)
-        for half, by in ((0, dg_), (1, du_)):
-            own[first + c, :, half] = dot(a[...], by[...], (0, 0)).astype(BF16).reshape(n, rows, COLS)
-        serve(*places, places[0] + 3 * c + 1)
-        by_down = dot(s_[...], dh[...], (0, 0)).astype(BF16)
+            held(h, 0, t)[...] = (silu * up).astype(BF16)
+            held(h, 2, t)[...] = (ds * silu).astype(BF16)
+            held(h, 1, t)[...] = (ds * up * (sig + silu * (1.0 - sig))).astype(BF16)
+
+    def gate_and_up(p, h):
+        for half in (0, 1):
+            own[p, :, half] = dot(a[...], held(h, 1 + half)[...], (0, 0)).astype(BF16).reshape(n, rows, COLS)
+
+    def down(l, c, h):
+        by_down = dot(held(h, 0)[...], dh[...], (0, 0)).astype(BF16)
         for g in range(COLS // plan.strip):
             group = c * (COLS // plan.strip) + g
             b, s = lax.div(group, plan.strips), lax.rem(group, plan.strips)
@@ -270,46 +267,57 @@
                 own[lax.div(i, 2), b, lax.rem(i, 2), f * plan.strip : (f + 1) * plan.strip] = by_down[
                     g * plan.strip : (g + 1) * plan.strip, f * COLS : (f + 1) * COLS
                 ]
-        serve(*places, places[0] + 3 * c + 2)
 
     pl.semaphore_wait(barrier, n - 1)
     squares[...] = jnp.zeros_like(squares)
 
-    def store(c):
-        return pltpu.make_async_copy(pairs[0], stash.at[c], stash_sems.at[2])
-
-    def fetch(c, pair):
-        return pltpu.make_async_copy(stash.at[chunk_of(2, c)], pairs[pair], stash_sems.at[pair])
-
-    places_1 = (0, 3 * chunks - 1)
-    places_in = (3 * chunks, 4 * chunks - 1)
-    place_norm = 4 * chunks
-    places_0 = (place_norm + 1, place_norm + 3 * chunks)
+    def store(c, h):
+        return pltpu.make_async_copy(sdd.at[h], stash.at[c], stash_sems.at[h])
+
+    def fetch(c, h):
+        return pltpu.make_async_copy(stash.at[c], sdd.at[h], stash_sems.at[h])
+
+    late = 2 * chunks
+    place_norm = late + chunks
+    places_0 = place_norm + 1
 
     @pl.loop(0, chunks)
     def _(c):
-        chunk_gradients(1, c, plan.at["gate", 1, 0] // 2, places_1)
+        slot, h = begin(1, c), lax.rem(c, 2)
+
+        @pl.when(c > 1)
+        def _():
+            store(c - 2, h).wait()
+
+        hidden(slot, h)
+
+        @pl.when(c + 1 < chunks)
+        def _():
+            store(c, h).start()
+
+        serve(0, late - 1, 2 * c)
+        gate_and_up(plan.at["gate", 1, 0] // 2 + c, h)
+        serve(0, late - 1, 2 * c + 1)
+
+    store(chunks - 2, (chunks - 2) % 2).wait()
 
     @pl.loop(0, chunks)
-    def _(c):
-        slot = begin(2, c)
-
-        def add(pair):
-            @pl.when(c > 0)
-            def _():
-                fetch(c, pair).wait()
-
-            @pl.when(c + 1 < chunks)
-            def _():
-                fetch(c + 1, 1 - pair).start()
-
-            by_gate, by_up = (pairs[pair].at[pl.ds(i * tokens, tokens)] for i in (0, 1))
-            for t in tiles:
-                add_to_acc(t, dot(by_gate[t], gate_buf[slot], (1, 1)) + dot(by_up[t], up_buf[slot], (1, 1)))
-
-        for pair in (0, 1):
-            pl.when(lax.rem(c, 2) == pair)(lambda pair=pair: add(pair))
-        serve(*places_in, places_in[0] + c)
+    def _(k):
+        slot, c = begin(2, k), chunk_of(2, k)
+        h = lax.rem(c, 2)
+
+        @pl.when(k > 0)
+        def _():
+            fetch(c, h).wait()
+
+        @pl.when(k + 1 < chunks)
+        def _():
+            fetch(chunk_of(2, k + 1), 1 - h).start()
+
+        for t in tiles:
+            add_to_acc(t, dot(held(h, 1, t)[...], gate_buf[slot], (1, 1)) + dot(held(h, 2, t)[...], up_buf[slot], (1, 1)))
+        down(1, c, h)
+        serve(late, place_norm - 1, late + k)
 
     again = pltpu.make_async_copy(x, a, in_sems.at[0])
     again.start()
@@ -326,10 +334,17 @@
 
     @pl.loop(0, chunks)
     def _(c):
-        chunk_gradients(3, c, plan.at["gate", 0, 0] // 2, places_0)
-
-    w_block, m_block, v_block = flat(sdd, rows), flat(mv, rows), flat(mv, rows, len(plan.subs))
-    held = len(plan.subs) * rows
+        last = places_0 + 3 * chunks - 1
+        hidden(begin(3, c), 0)
+        serve(places_0, last, places_0 + 3 * c)
+        gate_and_up(plan.at["gate", 0, 0] // 2 + c, 0)
+        serve(places_0, last, places_0 + 3 * c + 1)
+        down(0, c, 0)
+        serve(places_0, last, places_0 + 3 * c + 2)
+
+    w_rows = sdd.at[0]
+    w_block, m_block, v_block = flat(w_rows, rows), flat(mv, rows), flat(mv, rows, len(plan.subs))
+    mine = len(plan.subs) * rows
     for s, (block, arrays) in enumerate(((w_block, [b.at[:, me] for b in blocks]), (m_block, moments_m), (v_block, moments_v))):
         for i in range(len(plan.subs)):
             for inside, outside in plan.views(i, block, arrays):
@@ -337,12 +352,6 @@
 
     serve_late()
 
-    @pl.loop(0, units)
-    def _(p):
-        for h in range(hops):
-            for d in (0, 1):
-                hop(p, h, d).wait_send()
-
     folded = jnp.sum(squares[...].reshape(-1, 8, COLS), axis=0)
     sums[0] = sum(folded[:, i : i + 128] for i in range(0, COLS, 128))
 
@@ -353,7 +362,7 @@
 
     for k in range(1, n):
         tell(k).start()
-    for s, ref in enumerate((sdd.at[pl.ds(0, held)], mv.at[pl.ds(0, held)], mv.at[pl.ds(held, held)])):
+    for s, ref in enumerate((w_rows.at[pl.ds(0, mine)], mv.at[pl.ds(0, mine)], mv.at[pl.ds(mine, mine)])):
         pltpu.make_async_copy(ref, ref, state_sems.at[s]).wait()
     for k in range(1, n):
         tell(k).wait_recv()
@@ -373,11 +382,11 @@
     def _(p):
         for half in (0, 1):
             start = pl.multiple_of((2 * p + half) * rows, rows)
-            here, there = pl.ds(start, rows), pl.ds(start + held, rows)
+            here, there = pl.ds(start, rows), pl.ds(start + mine, rows)
             g = own[p, me, half].astype(F32) * factor
             m = 0.9 * mv[here] + 0.1 * g
             v = 0.95 * mv[there] + 0.05 * g * g
-            w = sdd[here].astype(F32)
+            w = w_rows[here].astype(F32)
             own[p, me, half] = (w - 0.02 * (m * lax.rsqrt(v + 1e-8) + 0.1 * w)).astype(BF16)
             mv[here] = m
             mv[there] = v
@@ -438,7 +447,7 @@
             step_kernel(plan, count, x, dy, weights, blocks, m, v, *refs[12:])
 
         results = [pltpu.VMEM((units, n, 2, rows, COLS), BF16), pltpu.VMEM((2 * subs * rows, COLS), F32)]
-        results += [jax.ShapeDtypeStruct((plan.chunks, 2 * tokens, COLS), BF16)]
+        results += [jax.ShapeDtypeStruct((plan.chunks, 3 * tokens, COLS), BF16)]
         own, mv, _ = pl.pallas_call(
             body,
             out_shape=results,
@@ -446,7 +455,7 @@
             out_specs=[in_vmem] * 2 + [anywhere],
             scratch_shapes=[pltpu.VMEM((tokens, d), BF16)] * 3
             + [
-                pltpu.VMEM((4 * tokens, COLS), BF16),
+                pltpu.VMEM((2, 3 * tokens, COLS), BF16),
                 pltpu.VMEM((2, d, COLS), BF16),
                 pltpu.VMEM((2, d, COLS), BF16),
                 pltpu.VMEM((2, COLS, d), BF16),
@@ -456,7 +465,7 @@
                 pltpu.VMEM((n, 8, 128), F32),
                 pltpu.SemaphoreType.DMA((tokens // TILE + 1,)),
                 pltpu.SemaphoreType.DMA((3, 2)),
-                pltpu.SemaphoreType.DMA((3,)),
+                pltpu.SemaphoreType.DMA((2,)),
                 pltpu.SemaphoreType.DMA((3,)),
                 pltpu.SemaphoreType.DMA((units, hops, 2)),
                 pltpu.SemaphoreType.DMA((units, hops, 2)),

time: 370 us -> 366 us (0.989)
  Pallas kernels: 369 us -> 365 us
    pallas_call x1, Pallas kernels: 361 us -> 357 us  [step(): pl.pallas_call(body, out_shape=results, in_specs=[anywhere] * 14, out_spe...]
where the time goes in v4:
time: 366 us
  Pallas kernels  365 us (100%)
    pallas_call x1, Pallas kernels, step(): pl.pallas_call(body, out_shape=results, in_specs=[anywhere] * 14, out_spe...  357 us
    pallas_call x1, Pallas kernels, step(): pl.pallas_call(place, out_shape=[jax.ShapeDtypeStruct(t.shape, t.dtype) f...  8.15 us

profile of v4, /device:TPU:28, one launch (start us, length us, event | category | flops | bytes accessed | tf_op | source)
XLA Modules:
  0.0 365.5 jit_solution(14286575423882775880)
XLA Ops:
  0.6 356.5 %step.1 = (bf16[21,8,2,96,256]{4,3,2,1,0:T(8,128)(2,1)S(1)}, f32[8064,256]{1,0:T(8,128)S(1)}, bf16[7,6144,256]{2,1,0:T(8,128)(2,1)}) custom-call(bf16[2048,768]{1,0:T(8,128)(2,1)} %bitcast.11, bf16[2048,768]{1,0:T(8,128)(2,1)} %bitcast.12, bf16[2,768,1792]{2,1,0:T(8,128)(2,1)} %refs_0_.1, bf16[2,768,1792]{2,1,0:T(8,128)(2,1)} %refs_1_.1, ...), custom_call_target="tpu_custom_call" | custom-call | tf_op jit(solution)/shard_map/step/pallas_call | solution.py:451
  357.2 8.2 %place.1 = (bf16[2,8,96,1792]{3,2,1,0:T(8,128)(2,1)}, bf16[2,8,96,1792]{3,2,1,0:T(8,128)(2,1)}, bf16[2,8,224,768]{3,2,1,0:T(8,128)(2,1)}, f32[2,96,1792]{2,1,0:T...) custom-call(bf16[21,8,2,96,256]{4,3,2,1,0:T(8,128)(2,1)S(1)} %get-tu, ...), custom_call_target="tpu_custom_call" | custom-call | tf_op jit(solution)/shard_map/place/pallas_call | solution.py:482

commit v5 on v4

--- a/solution.py
+++ b/solution.py
@@ -19,6 +19,9 @@
     (8, 9, 15, 17, 18, 19, 20, 28, 28, 30, 36, 37, 39, 42, *(LATE,) * 7),
     (12, 13, 19, 21, 22, 23, 24, 32, 32, 34, 40, 41, *(LATE,) * 9),
 )
+FIRST = 2
+EARLY = (4, 5)
+LEAD_NS = 12_000
 
 
 def dot(a, b, contract=(1, 0)):
@@ -83,8 +86,8 @@
 
 
 def step_kernel(plan, count, x, dy, weights, blocks, moments_m, moments_v, own, mv, stash, *scratch):
-    (x_buf, a, dh, sdd, gate_buf, up_buf, down_buf, half_landing, landing, squares, sums) = scratch[:11]
-    (in_sems, weight_sems, stash_sems, state_sems, send, recv, tell_send, tell_recv) = scratch[11:]
+    (x_buf, a, dh, sdd, gate_buf, up_buf, down_buf, half_landing, landing, squares, sums, state_0, g_0) = scratch[:13]
+    (in_sems, weight_sems, stash_sems, state_sems, send, recv, tell_send, tell_recv, moments_send, moments_recv, g_send, g_recv) = scratch[13:]
     n, hops, units, chunks, rows, tokens = plan.n, plan.hops, plan.units, plan.chunks, plan.rows, plan.tokens
     me = lax.axis_index("dp")
     right, left = lax.rem(me + 1, n), lax.rem(me + n - 1, n)
@@ -148,19 +151,44 @@
     load_dy = pltpu.make_async_copy(dy, dh, in_sems.at[len(tiles)])
     for copy in (loads[0], *weight_copies(0, 0, 0), *loads[1:]):
         copy.start()
-
-    for f in range(plan.folds):
-        acc[pl.ds(f * tokens, tokens)] = jnp.zeros((tokens, COLS), F32)
-    for t, load in zip(tiles, loads):
-        load.wait()
-        a[t] = normed(x_buf[t])
-    load_dy.start()
-
-    def forward(c, use):
+    for s, arrays in enumerate((moments_m, moments_v)):
+        for inside, outside in plan.views(0, lambda i, part, s=s: state_0.at[me, s, part], arrays):
+            pltpu.make_async_copy(outside, inside, state_sems.at[3]).start()
+
+
+    def to(d):
+        return {"dp": right if d == 0 else left}
+
+    def moments(q, h, d):
+        ref = state_0.at[at(-h) if d == 0 else at(h), q]
+        return pltpu.make_async_remote_copy(
+            ref, ref, moments_send.at[q, h, d], moments_recv.at[q, h, d], device_id=to(d), device_id_type=MESH
+        )
+
+    def move_moments(r):
+        h, q = 1 + lax.div(r, 2), lax.rem(r, 2)
+        for d in (0, 1):
+            moments(q, h - 1, d).wait_recv()
+            moments(q, h, d).start()
+
+    def move_last_moments(q):
+        moments(q, hops - 2, q).wait_recv()
+        moments(q, hops - 1, q).start()
+
+    def send_moments():
+        pl.semaphore_wait(barrier, n - 1)
+        pltpu.make_async_copy(state_0.at[me], state_0.at[me], state_sems.at[3]).wait()
+        for q in (0, 1):
+            for d in (0, 1):
+                moments(q, 0, d).start()
+
+    def forward(c, use, prepare=None):
         slot = begin(0, c)
         ready = None
         for t in (*tiles, None):
             if t is not None:
+                if prepare is not None:
+                    prepare(t)
                 gate, up = dot(a[t], gate_buf[slot]), dot(a[t], up_buf[slot])
                 after = t, (gate * sigmoid(gate) * up).astype(BF16)
             if ready is not None:
@@ -169,16 +197,32 @@
 
     def next_input(t, value):
         h = (x_buf[t].astype(F32) + (read_acc(t) + value).astype(BF16).astype(F32)).astype(BF16)
-        for f in range(plan.folds):
-            acc[part(f, t)] = jnp.zeros((TILE, COLS), F32)
         x_buf[t] = h
         a[t] = normed(h)
 
-    @pl.loop(0, chunks - 1)
+    def first_input(t):
+        a[t] = normed(x_buf[t])
+
+    def set_acc(t, value):
+        for f in range(plan.folds):
+            acc[part(f, t)] = value[:, f * COLS : (f + 1) * COLS]
+
+    for load in loads:
+        load.wait()
+    forward(0, set_acc, first_input)
+    load_dy.start()
+
+    @pl.loop(1, chunks - 1)
     def _(c):
+        pl.when(c == FIRST)(send_moments)
+        done = sum((c > at).astype(jnp.int32) for at in EARLY)
+        now = sum((c == at).astype(jnp.int32) for at in EARLY)
+        pl.loop(done, done + now)(move_moments)
         forward(c, add_to_acc)
 
+    move_moments(jnp.int32(2))
     forward(chunks - 1, next_input)
+    move_moments(jnp.int32(3))
     load_dy.wait()
 
     def hop(p, h, d):
@@ -232,9 +276,22 @@
                 else:
                     finish(p)
 
+    def spread(h, d):
+        ref = g_0.at[at(-h) if d == 0 else at(h)]
+        return pltpu.make_async_remote_copy(ref, ref, g_send.at[h, d], g_recv.at[h, d], device_id=to(d), device_id_type=MESH)
+
+    def spread_on(h):
+        for d in (0, 1):
+            if h > 0:
+                spread(h - 1, d).wait_recv()
+            if h < hops - 1 or d == 0:
+                spread(h, d).start()
+
     def serve_late():
         first = [sum(at < LATE for at in places) for places in HOPS]
         for h in range(hops + 1):
+            if h == hops:
+                spread_on(0)
 
             @pl.loop(first[h], units)
             def _(p, h=h):
@@ -268,7 +325,6 @@
                     g * plan.strip : (g + 1) * plan.strip, f * COLS : (f + 1) * COLS
                 ]
 
-    pl.semaphore_wait(barrier, n - 1)
     squares[...] = jnp.zeros_like(squares)
 
     def store(c, h):
@@ -295,11 +351,15 @@
         def _():
             store(c, h).start()
 
+        pl.when(c == 0)(lambda: move_last_moments(0))
         serve(0, late - 1, 2 * c)
         gate_and_up(plan.at["gate", 1, 0] // 2 + c, h)
+        pl.when(c == 0)(lambda: move_last_moments(1))
         serve(0, late - 1, 2 * c + 1)
 
     store(chunks - 2, (chunks - 2) % 2).wait()
+    for f in range(plan.folds):
+        acc[pl.ds(f * tokens, tokens)] = jnp.zeros((tokens, COLS), F32)
 
     @pl.loop(0, chunks)
     def _(k):
@@ -350,63 +410,117 @@
             for inside, outside in plan.views(i, block, arrays):
                 pltpu.make_async_copy(outside, inside, state_sems.at[s]).start()
 
+    w_0 = sdd.at[1, pl.ds(0, plan.d)]
+    _, l_0, c_0 = plan.subs[0]
+    pltpu.make_async_copy(weights[0].at[l_0, :, pl.ds(c_0 * COLS, COLS)], w_0, state_sems.at[3]).start()
+    g_0[me] = own[0, me, 0]
+
+    @pl.when(lax.rem(lax.axis_index("rep"), 2) == 0)
+    def _():
+        pl.delay(LEAD_NS)
+
     serve_late()
 
     folded = jnp.sum(squares[...].reshape(-1, 8, COLS), axis=0)
-    sums[0] = sum(folded[:, i : i + 128] for i in range(0, COLS, 128))
-
-    def tell(k):
+    sums[me] = sum(folded[:, i : i + 128] for i in range(0, COLS, 128))
+
+    def tell(k, b):
         return pltpu.make_async_remote_copy(
-            sums.at[0], sums.at[k], tell_send.at[k], tell_recv.at[k], device_id={"dp": at(k)}, device_id_type=MESH
+            sums.at[b], sums.at[b], tell_send.at[k], tell_recv.at[b], device_id={"dp": at(k)}, device_id_type=MESH
         )
 
     for k in range(1, n):
-        tell(k).start()
-    for s, ref in enumerate((w_rows.at[pl.ds(0, mine)], mv.at[pl.ds(0, mine)], mv.at[pl.ds(mine, mine)])):
+        tell(k, me).start()
+    spread_on(1)
+    for s, ref in enumerate((w_rows.at[pl.ds(0, mine)], mv.at[pl.ds(0, mine)], mv.at[pl.ds(mine, mine)], w_0)):
         pltpu.make_async_copy(ref, ref, state_sems.at[s]).wait()
+    spread_on(2)
     for k in range(1, n):
-        tell(k).wait_recv()
+        tell(k, at(k)).wait_recv()
     total = jnp.sum(jnp.sum(sums[...], axis=0), axis=(0, 1), keepdims=True)
     factor = jnp.minimum(1.0, 0.5 * lax.rsqrt(total / count + 1e-30))
     for k in range(1, n):
-        tell(k).wait_send()
+        tell(k, me).wait_send()
 
     def pass_on(p, h, d):
         b = at(-h) if d == 0 else at(h)
-        ref = own.at[p, b] if h < hops - 1 else own.at[p, b, d]
+        if isinstance(p, int):
+            ref = own.at[p, b, 1]
+        else:
+            ref = own.at[p, b] if h < hops - 1 else own.at[p, b, d]
         return pltpu.make_async_remote_copy(
             ref, ref, send.at[p, h, d], recv.at[p, h, d], device_id={"dp": right if d == 0 else left}, device_id_type=MESH
         )
 
-    @pl.loop(0, units)
+    def pass_first_on(h):
+        for d in (0, 1):
+            if h > 0:
+                pass_on(0, h - 1, d).wait_recv()
+            if h < hops - 1 or d == 1:
+                pass_on(0, h, d).start()
+
+    def stepped(w, m, v, g):
+        g = g.astype(F32) * factor
+        m = 0.9 * m + 0.1 * g
+        v = 0.95 * v + 0.05 * g * g
+        w = w.astype(F32)
+        return (w - 0.02 * (m * lax.rsqrt(v + 1e-8) + 0.1 * w)).astype(BF16), m, v
+
+    def take_step(p, half):
+        start = pl.multiple_of((2 * p + half) * rows, rows)
+        here, there = pl.ds(start, rows), pl.ds(start + mine, rows)
+        own[p, me, half], mv[here], mv[there] = stepped(w_rows[here], mv[here], mv[there], own[p, me, half])
+
+    @pl.loop(1, units)
     def _(p):
         for half in (0, 1):
-            start = pl.multiple_of((2 * p + half) * rows, rows)
-            here, there = pl.ds(start, rows), pl.ds(start + mine, rows)
-            g = own[p, me, half].astype(F32) * factor
-            m = 0.9 * mv[here] + 0.1 * g
-            v = 0.95 * mv[there] + 0.05 * g * g
-            w = w_rows[here].astype(F32)
-            own[p, me, half] = (w - 0.02 * (m * lax.rsqrt(v + 1e-8) + 0.1 * w)).astype(BF16)
-            mv[here] = m
-            mv[there] = v
+            take_step(p, half)
         for d in (0, 1):
             pass_on(p, 0, d).start()
 
+    for half in (0, 1):
+        take_step(0, half)
+    pass_first_on(0)
     for h in range(1, hops):
 
-        @pl.loop(0, units)
+        @pl.loop(1, units)
         def _(p, h=h):
             for d in (0, 1):
                 pass_on(p, h - 1, d).wait_recv()
                 pass_on(p, h, d).start()
 
-    @pl.loop(0, units)
+        pass_first_on(h)
+        if h == 1:
+            spread_on(hops - 1)
+        if h == 2:
+            spread(hops - 1, 0).wait_recv()
+            for k in range(hops):
+                for d in (0, 1):
+                    if k < hops - 1 or d == 0:
+                        spread(k, d).wait_send()
+                    for q in (0, 1):
+                        if k < hops - 1 or d == q:
+                            moments(q, k, d).wait_send()
+                        if (k == hops - 2 and d != q) or (k == hops - 1 and d == q):
+                            moments(q, k, d).wait_recv()
+
+            @pl.loop(0, n)
+            def _(b):
+                w = w_0[pl.ds(pl.multiple_of(b * rows, rows), rows)]
+                own[0, b, 0], _, _ = stepped(w, state_0[b, 0], state_0[b, 1], g_0[b])
+
+    @pl.loop(1, units)
     def _(p):
         for d in (0, 1):
             pass_on(p, hops - 1, d).wait_recv()
             for h in range(hops):
                 pass_on(p, h, d).wait_send()
+
+    pass_on(0, hops - 1, 1).wait_recv()
+    for h in range(hops):
+        for d in (0, 1):
+            if h < hops - 1 or d == 1:
+                pass_on(0, h, d).wait_send()
 
 
 def place_kernel(plan, own, mv, weights, new_m, new_v, sems):
@@ -463,16 +577,22 @@
                 pltpu.VMEM((units, 2, hops - 1, 2, rows, COLS), BF16),
                 pltpu.VMEM((rows, COLS), F32),
                 pltpu.VMEM((n, 8, 128), F32),
+                pltpu.VMEM((n, 2, rows, COLS), F32),
+                pltpu.VMEM((n, rows, COLS), BF16),
                 pltpu.SemaphoreType.DMA((tokens // TILE + 1,)),
                 pltpu.SemaphoreType.DMA((3, 2)),
                 pltpu.SemaphoreType.DMA((2,)),
-                pltpu.SemaphoreType.DMA((3,)),
+                pltpu.SemaphoreType.DMA((4,)),
                 pltpu.SemaphoreType.DMA((units, hops, 2)),
                 pltpu.SemaphoreType.DMA((units, hops, 2)),
                 pltpu.SemaphoreType.DMA((n,)),
                 pltpu.SemaphoreType.DMA((n,)),
+                pltpu.SemaphoreType.DMA((2, hops, 2)),
+                pltpu.SemaphoreType.DMA((2, hops, 2)),
+                pltpu.SemaphoreType.DMA((hops, 2)),
+                pltpu.SemaphoreType.DMA((hops, 2)),
             ],
-            compiler_params=pltpu.CompilerParams(collective_id=0, has_side_effects=True, vmem_limit_bytes=38 * 2**20),
+            compiler_params=pltpu.CompilerParams(collective_id=0, has_side_effects=True, vmem_limit_bytes=40 * 2**20),
             name="step",
         )(x[0], dy[0], *weights, *blocks, *m, *v)
 

time: 366 us -> 363 us (level)
  no operation moved by 1% of the time
where the time goes in v5:
time: 363 us; the launch traced here: 362 us
  Pallas kernels  362 us (100%)
    pallas_call x1, Pallas kernels, step(): pl.pallas_call(body, out_shape=results, in_specs=[anywhere] * 14, out_spe...  353 us
    pallas_call x1, Pallas kernels, step(): pl.pallas_call(place, out_shape=[jax.ShapeDtypeStruct(t.shape, t.dtype) f...  8.15 us

profile of v5, /device:TPU:28, one launch (start us, length us, event | category | flops | bytes accessed | tf_op | source)
XLA Modules:
  0.0 362.4 jit_solution(6108445963495442086)
XLA Ops:
  0.6 353.4 %step.1 = (bf16[21,8,2,96,256]{4,3,2,1,0:T(8,128)(2,1)S(1)}, f32[8064,256]{1,0:T(8,128)S(1)}, bf16[7,6144,256]{2,1,0:T(8,128)(2,1)}) custom-call(bf16[2048,768]{1,0:T(8,128)(2,1)} %bitcast.11, bf16[2048,768]{1,0:T(8,128)(2,1)} %bitcast.12, bf16[2,768,1792]{2,1,0:T(8,128)(2,1)} %refs_0_.1, bf16[2,768,1792]{2,1,0:T(8,128)(2,1)} %refs_1_.1, ...), custom_call_target="tpu_custom_call" | custom-call | tf_op jit(solution)/shard_map/step/pallas_call | solution.py:565
  354.1 8.2 %place.1 = (bf16[2,8,96,1792]{3,2,1,0:T(8,128)(2,1)}, bf16[2,8,96,1792]{3,2,1,0:T(8,128)(2,1)}, bf16[2,8,224,768]{3,2,1,0:T(8,128)(2,1)}, f32[2,96,1792]{2,1,0:T...) custom-call(bf16[21,8,2,96,256]{4,3,2,1,0:T(8,128)(2,1)S(1)} %get-tu, ...), custom_call_target="tpu_custom_call" | custom-call | tf_op jit(solution)/shard_map/place/pallas_call | solution.py:602

commit v6 on v4

--- a/solution.py
+++ b/solution.py
@@ -19,6 +19,7 @@
     (8, 9, 15, 17, 18, 19, 20, 28, 28, 30, 36, 37, 39, 42, *(LATE,) * 7),
     (12, 13, 19, 21, 22, 23, 24, 32, 32, 34, 40, 41, *(LATE,) * 9),
 )
+LEAD_NS = 19_000
 
 
 def dot(a, b, contract=(1, 0)):
@@ -82,8 +83,8 @@
     return lambda i, part: ref.at[pl.ds((first + i) * rows + part.start, part.size)]
 
 
-def step_kernel(plan, count, x, dy, weights, blocks, moments_m, moments_v, own, mv, stash, *scratch):
-    (x_buf, a, dh, sdd, gate_buf, up_buf, down_buf, half_landing, landing, squares, sums) = scratch[:11]
+def sums_kernel(plan, count, x, dy, weights, blocks, moments_m, moments_v, half_landing, mv, w_block, factor, stash, *scratch):
+    (x_buf, a, dh, sdd, gate_buf, up_buf, down_buf, own, landing, squares, sums) = scratch[:11]
     (in_sems, weight_sems, stash_sems, state_sems, send, recv, tell_send, tell_recv) = scratch[11:]
     n, hops, units, chunks, rows, tokens = plan.n, plan.hops, plan.units, plan.chunks, plan.rows, plan.tokens
     me = lax.axis_index("dp")
@@ -149,18 +150,14 @@
     for copy in (loads[0], *weight_copies(0, 0, 0), *loads[1:]):
         copy.start()
 
-    for f in range(plan.folds):
-        acc[pl.ds(f * tokens, tokens)] = jnp.zeros((tokens, COLS), F32)
-    for t, load in zip(tiles, loads):
-        load.wait()
-        a[t] = normed(x_buf[t])
-    load_dy.start()
-
-    def forward(c, use):
+
+    def forward(c, use, prepare=None):
         slot = begin(0, c)
         ready = None
         for t in (*tiles, None):
             if t is not None:
+                if prepare is not None:
+                    prepare(t)
                 gate, up = dot(a[t], gate_buf[slot]), dot(a[t], up_buf[slot])
                 after = t, (gate * sigmoid(gate) * up).astype(BF16)
             if ready is not None:
@@ -169,12 +166,22 @@
 
     def next_input(t, value):
         h = (x_buf[t].astype(F32) + (read_acc(t) + value).astype(BF16).astype(F32)).astype(BF16)
-        for f in range(plan.folds):
-            acc[part(f, t)] = jnp.zeros((TILE, COLS), F32)
         x_buf[t] = h
         a[t] = normed(h)
 
-    @pl.loop(0, chunks - 1)
+    def first_input(t):
+        a[t] = normed(x_buf[t])
+
+    def set_acc(t, value):
+        for f in range(plan.folds):
+            acc[part(f, t)] = value[:, f * COLS : (f + 1) * COLS]
+
+    for load in loads:
+        load.wait()
+    forward(0, set_acc, first_input)
+    load_dy.start()
+
+    @pl.loop(1, chunks - 1)
     def _(c):
         forward(c, add_to_acc)
 
@@ -208,7 +215,7 @@
         for half in (0, 1):
             g = own[p, me, half].astype(F32) + landing[p, 0, hops - 2, half].astype(F32) + landing[p, 1, hops - 2, half].astype(F32)
             g = g.astype(BF16)
-            own[p, me, half] = g
+            half_landing[p, half] = g
             g = g.astype(F32)
             squares[...] += g * g
         for h in range(hops):
@@ -235,7 +242,6 @@
     def serve_late():
         first = [sum(at < LATE for at in places) for places in HOPS]
         for h in range(hops + 1):
-
             @pl.loop(first[h], units)
             def _(p, h=h):
                 if h < hops:
@@ -300,6 +306,8 @@
         serve(0, late - 1, 2 * c + 1)
 
     store(chunks - 2, (chunks - 2) % 2).wait()
+    for f in range(plan.folds):
+        acc[pl.ds(f * tokens, tokens)] = jnp.zeros((tokens, COLS), F32)
 
     @pl.loop(0, chunks)
     def _(k):
@@ -342,56 +350,100 @@
         down(0, c, 0)
         serve(places_0, last, places_0 + 3 * c + 2)
 
-    w_rows = sdd.at[0]
-    w_block, m_block, v_block = flat(w_rows, rows), flat(mv, rows), flat(mv, rows, len(plan.subs))
-    mine = len(plan.subs) * rows
-    for s, (block, arrays) in enumerate(((w_block, [b.at[:, me] for b in blocks]), (m_block, moments_m), (v_block, moments_v))):
+    own_blocks = (
+        (flat(mv, rows), moments_m),
+        (flat(mv, rows, len(plan.subs)), moments_v),
+        (flat(w_block, rows), [b.at[:, me] for b in blocks]),
+    )
+    for s, (block, arrays) in enumerate(own_blocks):
         for i in range(len(plan.subs)):
             for inside, outside in plan.views(i, block, arrays):
                 pltpu.make_async_copy(outside, inside, state_sems.at[s]).start()
 
+    @pl.when(lax.rem(lax.axis_index("rep"), 2) == 0)
+    def _():
+        pl.delay(LEAD_NS)
+
     serve_late()
 
     folded = jnp.sum(squares[...].reshape(-1, 8, COLS), axis=0)
-    sums[0] = sum(folded[:, i : i + 128] for i in range(0, COLS, 128))
-
-    def tell(k):
+    sums[me] = sum(folded[:, i : i + 128] for i in range(0, COLS, 128))
+
+    def tell(k, b):
         return pltpu.make_async_remote_copy(
-            sums.at[0], sums.at[k], tell_send.at[k], tell_recv.at[k], device_id={"dp": at(k)}, device_id_type=MESH
+            sums.at[b], sums.at[b], tell_send.at[k], tell_recv.at[b], device_id={"dp": at(k)}, device_id_type=MESH
         )
 
     for k in range(1, n):
-        tell(k).start()
-    for s, ref in enumerate((w_rows.at[pl.ds(0, mine)], mv.at[pl.ds(0, mine)], mv.at[pl.ds(mine, mine)])):
+        tell(k, me).start()
+    mine = len(plan.subs) * rows
+    for s, ref in enumerate((mv.at[pl.ds(0, mine)], mv.at[pl.ds(mine, mine)], w_block)):
         pltpu.make_async_copy(ref, ref, state_sems.at[s]).wait()
     for k in range(1, n):
-        tell(k).wait_recv()
+        tell(k, at(k)).wait_recv()
     total = jnp.sum(jnp.sum(sums[...], axis=0), axis=(0, 1), keepdims=True)
-    factor = jnp.minimum(1.0, 0.5 * lax.rsqrt(total / count + 1e-30))
+    factor[...] = jnp.broadcast_to(jnp.minimum(1.0, 0.5 * lax.rsqrt(total / count + 1e-30)), factor.shape)
     for k in range(1, n):
-        tell(k).wait_send()
+        tell(k, me).wait_send()
+
+
+def update_kernel(plan, g, mv, w, factor, new_w, moments_m, moments_v, new_mv, out_sems):
+    rows, subs = plan.rows, len(plan.subs)
+    scale = factor[0:1, 0:1]
+    copies = []
+    for first in range(0, plan.units, 3):
+
+        @pl.loop(first, first + 3)
+        def _(p):
+            for half in (0, 1):
+                start = pl.multiple_of((2 * p + half) * rows, rows)
+                here, there = pl.ds(start, rows), pl.ds(start + subs * rows, rows)
+                by = g[p, half].astype(F32) * scale
+                m = 0.9 * mv[here] + 0.1 * by
+                v = 0.95 * mv[there] + 0.05 * by * by
+                old = w[here].astype(F32)
+                new_w[p, half] = (old - 0.02 * (m * lax.rsqrt(v + 1e-8) + 0.1 * old)).astype(BF16)
+                new_mv[here] = m
+                new_mv[there] = v
+
+        for i in range(2 * first, 2 * (first + 3)):
+            for s, (shift, arrays) in enumerate(((0, moments_m), (subs, moments_v))):
+                for views in plan.views(i, flat(new_mv, rows, shift), arrays):
+                    copies.append(pltpu.make_async_copy(*views, out_sems.at[s]))
+                    copies[-1].start()
+    for copy in copies:
+        copy.wait()
+
+
+def gather_kernel(plan, new_w, own, send, recv):
+    n, hops, units = plan.n, plan.hops, plan.units
+    me = lax.axis_index("dp")
+    right, left = lax.rem(me + 1, n), lax.rem(me + n - 1, n)
+    barrier = pltpu.get_barrier_semaphore()
+    for to in (right, left):
+        pl.semaphore_signal(barrier, inc=1, device_id={"dp": to}, device_id_type=MESH)
+    pl.semaphore_wait(barrier, 2)
 
     def pass_on(p, h, d):
-        b = at(-h) if d == 0 else at(h)
-        ref = own.at[p, b] if h < hops - 1 else own.at[p, b, d]
+        b = lax.rem(me - h + n, n) if d == 0 else lax.rem(me + h, n)
+        target = own.at[p, b] if h < hops - 1 else own.at[p, b, d]
         return pltpu.make_async_remote_copy(
-            ref, ref, send.at[p, h, d], recv.at[p, h, d], device_id={"dp": right if d == 0 else left}, device_id_type=MESH
+            new_w.at[p] if h == 0 else target,
+            target,
+            send.at[p, h, d],
+            recv.at[p, h, d],
+            device_id={"dp": right if d == 0 else left},
+            device_id_type=MESH,
         )
 
     @pl.loop(0, units)
     def _(p):
-        for half in (0, 1):
-            start = pl.multiple_of((2 * p + half) * rows, rows)
-            here, there = pl.ds(start, rows), pl.ds(start + mine, rows)
-            g = own[p, me, half].astype(F32) * factor
-            m = 0.9 * mv[here] + 0.1 * g
-            v = 0.95 * mv[there] + 0.05 * g * g
-            w = w_rows[here].astype(F32)
-            own[p, me, half] = (w - 0.02 * (m * lax.rsqrt(v + 1e-8) + 0.1 * w)).astype(BF16)
-            mv[here] = m
-            mv[there] = v
         for d in (0, 1):
             pass_on(p, 0, d).start()
+
+    @pl.loop(0, units)
+    def _(p):
+        own[p, me] = new_w[p]
 
     for h in range(1, hops):
 
@@ -409,20 +461,11 @@
                 pass_on(p, h, d).wait_send()
 
 
-def place_kernel(plan, own, mv, weights, new_m, new_v, sems):
+def place_kernel(plan, own, weights, sem):
     def gathered(i, part):
         return own.at[i // 2, :, i % 2, part]
 
-    copies = []
-    for i in range(len(plan.subs)):
-        for s, (block, arrays, lead) in enumerate(
-            (
-                (gathered, weights, (EVERY,)),
-                (flat(mv, plan.rows), new_m, ()),
-                (flat(mv, plan.rows, len(plan.subs)), new_v, ()),
-            )
-        ):
-            copies += [pltpu.make_async_copy(*views, sems.at[s]) for views in plan.views(i, block, arrays, lead)]
+    copies = [pltpu.make_async_copy(*views, sem) for i in range(len(plan.subs)) for views in plan.views(i, gathered, weights, (EVERY,))]
     for copy in copies:
         copy.start()
     for copy in copies:
@@ -442,24 +485,40 @@
         units, rows, hops, subs = plan.units, plan.rows, plan.hops, len(plan.subs)
         anywhere, in_vmem = pl.BlockSpec(memory_space=pl.ANY), pl.BlockSpec(memory_space=pltpu.VMEM)
 
-        def body(x, dy, *refs):
-            weights, blocks, m, v = (refs[i : i + 3] for i in (0, 3, 6, 9))
-            step_kernel(plan, count, x, dy, weights, blocks, m, v, *refs[12:])
-
-        results = [pltpu.VMEM((units, n, 2, rows, COLS), BF16), pltpu.VMEM((2 * subs * rows, COLS), F32)]
-        results += [jax.ShapeDtypeStruct((plan.chunks, 3 * tokens, COLS), BF16)]
-        own, mv, _ = pl.pallas_call(
-            body,
-            out_shape=results,
-            in_specs=[anywhere] * 14,
-            out_specs=[in_vmem] * 2 + [anywhere],
-            scratch_shapes=[pltpu.VMEM((tokens, d), BF16)] * 3
+        assert units % 3 == 0
+        unit = (units, 2, rows, COLS)
+        flat_moments = pltpu.VMEM((2 * subs * rows, COLS), F32)
+
+        def call(kernel, name, results, operands, spaces, out_spaces, scratch, limit, remote=None):
+            params = {} if remote is None else {"collective_id": remote, "has_side_effects": True}
+            return pl.pallas_call(
+                kernel,
+                out_shape=results,
+                in_specs=spaces,
+                out_specs=out_spaces,
+                scratch_shapes=scratch,
+                compiler_params=pltpu.CompilerParams(vmem_limit_bytes=limit * 2**20, **params),
+                name=name,
+            )(*operands)
+
+        def sums(x, dy, *refs):
+            sums_kernel(plan, count, x, dy, *(refs[i : i + 3] for i in (0, 3, 6, 9)), *refs[12:])
+
+        g, mv, w_block, factor, _ = call(
+            sums,
+            "sums",
+            [pltpu.VMEM(unit, BF16), flat_moments, pltpu.VMEM((subs * rows, COLS), BF16), pltpu.VMEM((8, 128), F32)]
+            + [jax.ShapeDtypeStruct((plan.chunks, 3 * tokens, COLS), BF16)],
+            (x[0], dy[0], *weights, *blocks, *m, *v),
+            [anywhere] * 14,
+            [in_vmem] * 4 + [anywhere],
+            [pltpu.VMEM((tokens, d), BF16)] * 3
             + [
                 pltpu.VMEM((2, 3 * tokens, COLS), BF16),
                 pltpu.VMEM((2, d, COLS), BF16),
                 pltpu.VMEM((2, d, COLS), BF16),
                 pltpu.VMEM((2, COLS, d), BF16),
-                pltpu.VMEM((units, 2, rows, COLS), BF16),
+                pltpu.VMEM((units, n, 2, rows, COLS), BF16),
                 pltpu.VMEM((units, 2, hops - 1, 2, rows, COLS), BF16),
                 pltpu.VMEM((rows, COLS), F32),
                 pltpu.VMEM((n, 8, 128), F32),
@@ -472,23 +531,53 @@
                 pltpu.SemaphoreType.DMA((n,)),
                 pltpu.SemaphoreType.DMA((n,)),
             ],
-            compiler_params=pltpu.CompilerParams(collective_id=0, has_side_effects=True, vmem_limit_bytes=38 * 2**20),
-            name="step",
-        )(x[0], dy[0], *weights, *blocks, *m, *v)
-
-        def place(*refs):
-            place_kernel(plan, *refs[:2], refs[2:5], refs[5:8], refs[8:11], refs[11])
-
-        out = pl.pallas_call(
+            51,
+            remote=0,
+        )
+
+        def update(*refs):
+            update_kernel(plan, *refs[:5], refs[5:8], refs[8:11], *refs[11:])
+
+        new_w, *new_moments = call(
+            update,
+            "update",
+            [pltpu.VMEM(unit, BF16)] + [jax.ShapeDtypeStruct(t.shape, t.dtype) for t in (*m, *v)],
+            (g, mv, w_block, factor),
+            [in_vmem] * 4,
+            [in_vmem] + [anywhere] * 6,
+            [flat_moments, pltpu.SemaphoreType.DMA((2,))],
+            10,
+        )
+
+        def gather(*refs):
+            gather_kernel(plan, *refs)
+
+        own = call(
+            gather,
+            "gather",
+            pltpu.VMEM((units, n, 2, rows, COLS), BF16),
+            (new_w,),
+            [in_vmem],
+            in_vmem,
+            [pltpu.SemaphoreType.DMA((units, hops, 2)), pltpu.SemaphoreType.DMA((units, hops, 2))],
+            2,
+            remote=1,
+        )
+
+        def place(own, *refs):
+            place_kernel(plan, own, refs[:3], refs[3])
+
+        new_weights = call(
             place,
-            out_shape=[jax.ShapeDtypeStruct(t.shape, t.dtype) for t in (*blocks, *m, *v)],
-            in_specs=[in_vmem] * 2,
-            out_specs=[anywhere] * 9,
-            scratch_shapes=[pltpu.SemaphoreType.DMA((3,))],
-            compiler_params=pltpu.CompilerParams(vmem_limit_bytes=2**20),
-            name="place",
-        )(own, mv)
-        return tuple(o.reshape(w.shape) for o, w in zip(out[:3], weights)) + tuple(out[3:])
+            "place",
+            [jax.ShapeDtypeStruct(t.shape, t.dtype) for t in blocks],
+            (own,),
+            [in_vmem],
+            [anywhere] * 3,
+            [pltpu.SemaphoreType.DMA],
+            1,
+        )
+        return tuple(o.reshape(w.shape) for o, w in zip(new_weights, weights)) + tuple(new_moments)
 
     block = P(None, "dp", None)
     sequence = P(("rep", "dp"), None, None)

time: 366 us -> 359 us (0.981)
  Pallas kernels: 365 us -> 358 us
    pallas_call x2 -> x4, Pallas kernels: 365 us -> 358 us  [call(): pl.pallas_call(kernel, out_shape=results, in_specs=spaces, out_specs=out_...]
where the time goes in v6:
time: 359 us
  Pallas kernels  358 us (100%)
    pallas_call x4, Pallas kernels, call(): pl.pallas_call(kernel, out_shape=results, in_specs=spaces, out_specs=out_...  358 us

profile of v6, /device:TPU:28, one launch (start us, length us, event | category | flops | bytes accessed | tf_op | source)
XLA Modules:
  0.0 358.7 jit_solution(2466185223318161003)
XLA Ops:
  0.6 202.8 %sums.1 = (bf16[21,2,96,256]{3,2,1,0:T(8,128)(2,1)S(1)}, f32[8064,256]{1,0:T(8,128)S(1)}, bf16[4032,256]{1,0:T(8,128)(2,1)S(1)}, f32[8,128]{1,0:T(8,128)S(1)}, bf16[7,6144,256]{2,1,0:T(8,128)(2,1)}) custom-call(bf16[2048,768]{1,0:T(8,128)(2,1)} %bitcast.11, bf16[2048,768]{1,0:T(8,128)(2,1)} %bitcast.12, bf16[2,768,1792]{2,1,0:T(8,128)(2,1)} %refs_0_.1, ...), custom_call_target="tpu_custom_call" | custom-call | tf_op jit(solution)/shard_map/sums/pallas_call | solution.py:494
  203.5 3.9 %update.1 = (bf16[21,2,96,256]{3,2,1,0:T(8,128)(2,1)S(1)}, f32[2,96,1792]{2,1,0:T(8,128)}, f32[2,96,1792]{2,1,0:T(8,128)}, f32[2,224,768]{2,1,0:T(8,128)}, f32[2...) custom-call(bf16[21,2,96,256]{3,2,1,0:T(8,128)(2,1)S(1)} %get-tuple-element.23.refs_0_, ...), custom_call_target="tpu_custom_call" | custom-call | tf_op jit(solution)/shard_map/update/pallas_call | solution.py:494
  207.4 145.4 %gather.1.own = bf16[21,8,2,96,256]{4,3,2,1,0:T(8,128)(2,1)S(1)} custom-call(bf16[21,2,96,256]{3,2,1,0:T(8,128)(2,1)S(1)} %get-tuple-element.27.refs_0_), custom_call_target="tpu_custom_call" | custom-call | tf_op jit(solution)/shard_map/gather/pallas_call | solution.py:494
  352.8 5.7 %place.1 = (bf16[2,8,96,1792]{3,2,1,0:T(8,128)(2,1)}, bf16[2,8,96,1792]{3,2,1,0:T(8,128)(2,1)}, bf16[2,8,224,768]{3,2,1,0:T(8,128)(2,1)}) custom-call(bf16[21,8,2,96,256]{4,3,2,1,0:T(8,128)(2,1)S(1)} %gather.1.own), custom_call_target="tpu_custom_call" | custom-call | tf_op jit(solution)/shard_map/place/pallas_call | solution.py:494

commit v7 on v6

--- a/solution.py
+++ b/solution.py
@@ -19,7 +19,7 @@
     (8, 9, 15, 17, 18, 19, 20, 28, 28, 30, 36, 37, 39, 42, *(LATE,) * 7),
     (12, 13, 19, 21, 22, 23, 24, 32, 32, 34, 40, 41, *(LATE,) * 9),
 )
-LEAD_NS = 19_000
+LEAD_NS = 21_000
 
 
 def dot(a, b, contract=(1, 0)):

time: 359 us -> 359 us (level)
  no operation moved by 1% of the time
where the time goes in v7:
time: 359 us
  Pallas kernels  358 us (100%)
    pallas_call x4, Pallas kernels, call(): pl.pallas_call(kernel, out_shape=results, in_specs=spaces, out_specs=out_...  358 us

profile of v7, /device:TPU:28, one launch (start us, length us, event | category | flops | bytes accessed | tf_op | source)
XLA Modules:
  0.0 358.7 jit_solution(307575615336573555)
XLA Ops:
  0.6 204.8 %sums.1 = (bf16[21,2,96,256]{3,2,1,0:T(8,128)(2,1)S(1)}, f32[8064,256]{1,0:T(8,128)S(1)}, bf16[4032,256]{1,0:T(8,128)(2,1)S(1)}, f32[8,128]{1,0:T(8,128)S(1)}, bf16[7,6144,256]{2,1,0:T(8,128)(2,1)}) custom-call(bf16[2048,768]{1,0:T(8,128)(2,1)} %bitcast.11, bf16[2048,768]{1,0:T(8,128)(2,1)} %bitcast.12, bf16[2,768,1792]{2,1,0:T(8,128)(2,1)} %refs_0_.1, ...), custom_call_target="tpu_custom_call" | custom-call | tf_op jit(solution)/shard_map/sums/pallas_call | solution.py:494
  205.5 3.9 %update.1 = (bf16[21,2,96,256]{3,2,1,0:T(8,128)(2,1)S(1)}, f32[2,96,1792]{2,1,0:T(8,128)}, f32[2,96,1792]{2,1,0:T(8,128)}, f32[2,224,768]{2,1,0:T(8,128)}, f32[2...) custom-call(bf16[21,2,96,256]{3,2,1,0:T(8,128)(2,1)S(1)} %get-tuple-element.23.refs_0_, ...), custom_call_target="tpu_custom_call" | custom-call | tf_op jit(solution)/shard_map/update/pallas_call | solution.py:494
  209.4 143.4 %gather.1.own = bf16[21,8,2,96,256]{4,3,2,1,0:T(8,128)(2,1)S(1)} custom-call(bf16[21,2,96,256]{3,2,1,0:T(8,128)(2,1)S(1)} %get-tuple-element.27.refs_0_), custom_call_target="tpu_custom_call" | custom-call | tf_op jit(solution)/shard_map/gather/pallas_call | solution.py:494
  352.8 5.7 %place.1 = (bf16[2,8,96,1792]{3,2,1,0:T(8,128)(2,1)}, bf16[2,8,96,1792]{3,2,1,0:T(8,128)(2,1)}, bf16[2,8,224,768]{3,2,1,0:T(8,128)(2,1)}) custom-call(bf16[21,8,2,96,256]{4,3,2,1,0:T(8,128)(2,1)S(1)} %gather.1.own), custom_call_target="tpu_custom_call" | custom-call | tf_op jit(solution)/shard_map/place/pallas_call | solution.py:494
